TPU v7x, 256 devices: a whole 4x4x8 slice. The times are simulated.
256 devices in a mesh: row: 8 (over z), col: 32 (over x, y, core).
Axes of the slice: x: 4, y: 4, z: 8, core: 2. Of those that a mesh axis runs over, the one named last changes fastest.
Arguments:
- rho_real: float32 [4096, 4096], P('row', 'col'), may hold values from -2.5 to 4, as said below
- rho_imag: float32 [4096, 4096], P('row', 'col'), may hold values from -2.5 to 2.5, as said below
- hamiltonian: bfloat16 [4096, 4096], P('row', 'col'), may hold values from -1 to 1
- amplitudes: float32 [8, 4096], replicated, may hold values from 0.15 to 0.6
- offsets: int32 [8], replicated, may hold values from -16 to 16
- active_jumps: int32 [1], replicated, may hold values from 4 to 8
Outputs:
- rho_next_real: float32 [4096, 4096], P('row', 'col')
- rho_next_imag: float32 [4096, 4096], P('row', 'col')
Inputs may be any that keep to these rules, and one draw needn't show every extreme that they name: `rho_real`: symmetric, with every diagonal entry 0.5 or more. `rho_imag`: antisymmetric.
All inputs are finite; a program needn't handle non-finite values.
Results may differ from a plain program's by a relative error of at most 0.001.
Values may be sent and summed in bfloat16 or wider, within the bound.
A program may use at most 64 MiB of HBM per device.

v0:
```python
import jax
import jax.numpy as jnp
from jax import lax
from jax.sharding import Mesh
from jax.sharding import PartitionSpec as P

OMAX = 16
COL = ("col_0", "col_1", "col_2")
ROW_COL = ("row", "col_0", "col_1", "col_2")


step_size = 0.25


def in_order(tiles, dim):
    lengths = list(tiles.shape[1:])
    lengths[dim] *= tiles.shape[0]
    return jnp.moveaxis(tiles, 0, dim).reshape(lengths)


def sent_to_all(x, axis):
    peers = lax.axis_size(axis)
    return lax.all_to_all(jnp.broadcast_to(x[None], (peers, *x.shape)), axis, 0, 0, tiled=True)


def gathered_copies(x, axis, dim):
    return in_order(sent_to_all(x, axis), dim)


def by_axis(x, axes):
    for axis in axes:
        x = lax.psum(x, axis)
    return x


def in_one_piece(arrays, axis, dim, along):
    both = jnp.concatenate(arrays, axis=along)
    out, at, finished = (gathered_copies(both, axis, dim), 0, [])
    for a in arrays:
        finished.append(lax.slice_in_dim(out, at, at + a.shape[along], axis=along))
        at += a.shape[along]
    return tuple(finished)


def sent_together(arrays, axis, dim, along):
    both = jnp.concatenate(arrays, axis=along)
    out, at, finished = (lax.all_gather(both, axis, axis=dim, tiled=True), 0, [])
    for a in arrays:
        finished.append(lax.slice_in_dim(out, at, at + a.shape[along], axis=along))
        at += a.shape[along]
    return tuple(finished)


def extended(cells, sides, width):
    for axis, dim in sides:
        count = lax.axis_size(axis)
        ends = count - 1
        head = lax.slice_in_dim(cells, 0, width, axis=dim)
        tail = lax.slice_in_dim(cells, cells.shape[dim] - width, cells.shape[dim], axis=dim)
        cells = jnp.concatenate(
            [
                lax.ppermute(tail, axis, [(i, (i + 1) % count) for i in range(ends)]),
                cells,
                lax.ppermute(head, axis, [((i + 1) % count, i) for i in range(ends)]),
            ],
            axis=dim,
        )
    return cells


def dissipate(matrix, padded, amplitudes, offsets, active, row_first, col_first):
    height = matrix.shape[1]
    breadth = matrix.shape[2]
    levels = amplitudes.shape[1]
    margin = (padded.shape[1] - height) // 2
    positions = jnp.arange(levels, dtype=jnp.int32)
    summed = jnp.zeros(matrix.shape, matrix.dtype)
    for jump_slot in range(amplitudes.shape[0]):
        offset = offsets[jump_slot]
        inside = (positions + offset >= 0) & (positions + offset < levels)
        strength = jnp.where(inside, amplitudes[jump_slot], 0.0)
        outflow = jnp.pad(strength * strength, (margin, margin))
        outflow = lax.dynamic_slice_in_dim(outflow, margin - offset, levels)
        row_strength = lax.dynamic_slice_in_dim(strength, row_first, height)
        col_strength = lax.dynamic_slice_in_dim(strength, col_first, breadth)
        row_outflow = lax.dynamic_slice_in_dim(outflow, row_first, height)
        col_outflow = lax.dynamic_slice_in_dim(outflow, col_first, breadth)
        corner = margin + offset
        shifted = lax.dynamic_slice(padded, (jnp.int32(0), corner, corner), (2, height, breadth))
        contribution = (
            row_strength[:, None] * col_strength[None, :] * shifted
            - 0.5 * (row_outflow[:, None] + col_outflow[None, :]) * matrix
        )
        summed = summed + jnp.where(jump_slot < active, contribution, 0.0)
    return summed


def diagonal_sum(matrix, row_first, col_first):
    row_index = lax.broadcasted_iota(jnp.int32, matrix.shape, 0) + row_first
    col_index = lax.broadcasted_iota(jnp.int32, matrix.shape, 1) + col_first
    return jnp.sum(jnp.where(row_index == col_index, matrix, 0.0))


def local(rho_real, rho_imag, hamiltonian, amplitudes, offsets, active_jumps):
    height, breadth = rho_real.shape
    levels = amplitudes.shape[1]
    row_first = lax.axis_index("row") * height
    col_first = lax.axis_index(COL) * breadth
    active = active_jumps[0]
    ham_columns = gathered_copies(hamiltonian, "row", 0)
    start_trace = by_axis(diagonal_sum(rho_real, row_first, col_first), ROW_COL)

    def drift(real_part, imag_part):
        real_low = real_part.astype(jnp.bfloat16)
        imag_low = imag_part.astype(jnp.bfloat16)
        row_panel = lax.all_gather(hamiltonian, COL, axis=1, tiled=True)
        pieces = in_one_piece((real_low, imag_low), "row", 0, 1)
        strip = row_panel
        left_real = jnp.dot(strip, pieces[0], preferred_element_type=jnp.float32)
        left_imag = jnp.dot(strip, pieces[1], preferred_element_type=jnp.float32)
        pieces = sent_together((real_low, imag_low), COL, 1, 0)
        strip = ham_columns
        right_real = jnp.dot(pieces[0], strip, preferred_element_type=jnp.float32)
        right_imag = jnp.dot(pieces[1], strip, preferred_element_type=jnp.float32)
        matrix = jnp.stack([real_part, imag_part])
        padded = extended(matrix.astype(jnp.bfloat16), (("row", 1), (COL, 2)), OMAX).astype(
            matrix.dtype
        )
        loss = dissipate(matrix, padded, amplitudes, offsets, active, row_first, col_first)
        return (left_imag - right_imag + loss[0], right_real - left_real + loss[1])

    first_real, first_imag = drift(rho_real, rho_imag)
    middle_real = rho_real + step_size * first_real
    middle_imag = rho_imag + step_size * first_imag
    rescale = levels / start_trace
    middle_real = middle_real * rescale
    middle_imag = middle_imag * rescale
    second_real, second_imag = drift(middle_real, middle_imag)
    updated_real = rho_real + 0.5 * step_size * (first_real + second_real)
    updated_imag = rho_imag + 0.5 * step_size * (first_imag + second_imag)
    rescale = levels / start_trace
    return (updated_real * rescale, updated_imag * rescale)


def solution(mesh):
    split = Mesh(
        mesh.devices.reshape(mesh.shape["row"], 4, 4, 2), ("row", "col_0", "col_1", "col_2")
    )
    placed = (P("row", COL), P("row", COL), P("row", COL), P(), P(), P())
    return jax.shard_map(
        local,
        mesh=split,
        in_specs=placed,
        out_specs=(P("row", COL), P("row", COL)),
        check_vma=False,
    )
```

profile of v0, /device:TPU:25, one launch (start us, length us, event | category | flops | bytes accessed | tf_op | source)
XLA Modules:
  0.0 268.6 jit_solution(7100053074104402569)
XLA Ops:
  7.3 1.0 convert_element_type.42
  8.2 1.8 select_reduce_fusion
  10.0 0.7 pad_maximum_fusion.3
  10.8 0.7 all-gather.4.cloned.1.call-update
  11.5 1.1 copy.16
  12.6 1.1 copy.10
  13.7 0.7 fusion.83
  14.4 3.5 %collective-permute-start = (bf16[2,16,128]{1,2,0:T(8,128)(2,1)}, bf16[2,16,128]{1,2,0:T(8,128)(2,1)S(1)}, u32[]{:S(2)}, u32[]{:S(2)}) collective-permute-start(bf16[2,16,128]{1,2,0:T(8,128)(2,1)} %get-tuple-element.32), channel_id=1, source_target_pairs={{0,32},{32,64},{64,96},{96,128},{128,160},{160,192},{192,224},{1,3... | collective-permute-start | bytes 24584 | tf_op jit(solution)/shard_map/ppermute | solution.py:62
  18.0 1.3 collective-permute-start.1
  19.3 2.0 broadcast_in_dim.49
  21.3 9.8 %all-to-all-start.1 = ((bf16[8,512,128]{2,1,0:T(8,128)(2,1)}), bf16[8,512,128]{2,1,0:T(8,128)(2,1)S(1)}, u32[]{:S(2)}, u32[]{:S(2)}) async-start(bf16[8,512,128]{2,1,0:T(8,128)(2,1)} %broadcast_in_dim.49), calls=%async_computation.1 | async-start | bytes 2097152 | tf_op jit(solution)/shard_map/all_to_all | solution.py:23
  31.1 0.7 fusion.85
  34.6 0.6 fusion.76
  35.9 0.7 fusion.66
  37.1 0.7 fusion.70
  38.4 27.6 %psum.28 = f32[]{:T(128)} all-reduce(f32[]{:T(128)} %get-tuple-element.30), channel_id=1, replica_groups=mesh['row'=8,'col_0'=4,'col_1'=4,'col_2'=2] {'row'}, use_global_device_ids=true, to_apply=%region_1.2 | all-reduce | flops 1 | bytes 8 | tf_op jit(solution)/shard_map/psum | solution.py:32
  72.4 0.7 pad_dynamic-slice_fusion.8
  73.0 0.7 pad_dynamic-slice_fusion.10
  74.3 0.7 pad_dynamic-slice_fusion.12
  75.0 0.6 fusion.80
  76.2 0.7 pad_dynamic-slice_fusion.5
  76.9 0.7 pad_dynamic-slice_fusion.15
  77.5 0.7 pad_dynamic-slice_fusion.9
  79.4 1.5 broadcast_in_dim.48
  81.1 4.2 %all-to-all-start = ((bf16[8,512,256]{2,1,0:T(8,128)(2,1)}), bf16[8,512,256]{2,1,0:T(8,128)(2,1)S(1)}, u32[]{:S(2)}, u32[]{:S(2)}) async-start(bf16[8,512,256]{2,1,0:T(8,128)(2,1)} %broadcast_in_dim.48), calls=%async_computation | async-start | bytes 4194304 | tf_op jit(solution)/shard_map/all_to_all | solution.py:23
  85.9 9.1 %psum.29 = f32[]{:T(128)} all-reduce(f32[]{:T(128)} %psum.28), channel_id=1, replica_groups=mesh['row'=8,'col_0'=4,'col_1'=4,'col_2'=2] {'col_0'}, use_global_device_ids=true, to_apply=%region_2.3 | all-reduce | flops 1 | bytes 8 | tf_op jit(solution)/shard_map/psum | solution.py:32
  97.6 0.7 pad_dynamic-slice_fusion.7
  98.4 1.5 add_multiply_fusion.2
  99.9 0.9 broadcast_multiply_fusion.6
  100.8 1.6 add_multiply_fusion.8
  102.4 0.9 broadcast_multiply_fusion.4
  103.3 1.6 add_multiply_fusion.6
  104.9 0.9 broadcast_multiply_fusion.2
  106.4 6.6 %psum.30 = f32[]{:T(128)} all-reduce(f32[]{:T(128)} %psum.29), channel_id=1, replica_groups=mesh['row'=8,'col_0'=4,'col_1'=4,'col_2'=2] {'col_1'}, use_global_device_ids=true, to_apply=%region_3.4 | all-reduce | flops 1 | bytes 8 | tf_op jit(solution)/shard_map/psum | solution.py:32
  113.0 0.7 pad_maximum_fusion.11
  113.7 11.7 %collective-permute-start.2 = (bf16[2,544,16]{1,2,0:T(8,128)(2,1)}, bf16[2,544,16]{1,2,0:T(8,128)(2,1)}, u32[]{:S(2)}, u32[]{:S(2)}) collective-permute-start(bf16[2,544,16]{1,2,0:T(8,128)(2,1)} %get-tuple-element.26), channel_id=1, source_target_pairs={{0,1},{1,2},{2,3},{3,4},{4,5},{5,6},{6,7},{7,8},{8,9},{9,10},{10,1... | collective-permute-start | bytes 104456 | tf_op jit(solution)/shard_map/ppermute | solution.py:62
  125.4 1.9 collective-permute-start.3
  127.3 1.6 add_multiply_fusion.4
  128.9 3.2 %psum.31 = f32[]{:T(128)} all-reduce(f32[]{:T(128)} %psum.30), channel_id=1, replica_groups=mesh['row'=8,'col_0'=4,'col_1'=4,'col_2'=2] {'col_2'}, use_global_device_ids=true, to_apply=%region_4.5 | all-reduce | flops 1 | bytes 8 | tf_op jit(solution)/shard_map/psum | solution.py:32
  148.6 1.0 maximum_convert_fusion
  149.5 4.5 %select_add_fusion.1 = f32[2,512,128]{1,2,0:T(8,128)} fusion(f32[2,544,160]{1,2,0:T(8,128)S(1)} %maximum_convert_fusion, s32[]{:T(128)S(6)} %select_n.358, s32[]{:T(128)S(6)} %select_n.359, s32[]{:T(128)S(6)} %select_n.351, s32[]{:T(128)S(6)} %select_n.352, s32[]{:T(128)S(6)} %select_n.344, s32[]{:T(128)S(6)} %select_n.345, s32[]{:T(128)S(6)} %select_n.337, ...), kind=kLoop, calls=%fused_computation.35 | loop fusion | flops 5242880 | bytes 9437256 | tf_op jit(solution)/shard_map/add | solution.py:94
  154.1 4.0 %fusion.6 = f32[512,128]{0,1:T(8,128)S(1)} fusion(bf16[4096,128]{1,0:T(8,128)(2,1)} %bitcast.105, bf16[1024,4096]{1,0:T(8,128)(2,1)} %all-gather.6.cloned.1.call-done), kind=kOutput, calls=%fused_computation.6 | convolution fusion | flops 536870912 | bytes 5505024 | tf_op jit(solution)/shard_map/dot_general | solution.py:124
  158.1 3.8 %fusion.9 = f32[512,128]{0,1:T(8,128)S(1)} fusion(f32[512,128]{0,1:T(8,128)S(1)} %fusion.6, bf16[512,4096]{1,0:T(8,128)(2,1)} %all-gather.4.cloned.1.call-done, bf16[4096,256]{1,0:T(8,128)(2,1)S(1)} %bitcast.97, f32[2,512,128]{1,2,0:T(8,128)} %select_add_fusion.1), kind=kOutput, calls=%fused_computation.13 | convolution fusion | flops 537001984 | bytes 6029312 | tf_op jit(solution)/shard_map/dot_general | solution.py:120
  162.0 0.7 copy-done.5
  162.8 3.8 %fusion.4 = f32[512,128]{0,1:T(8,128)S(1)} fusion(bf16[4096,128]{1,0:T(8,128)(2,1)S(1)} %bitcast.108, bf16[1024,4096]{1,0:T(8,128)(2,1)} %all-gather.6.cloned.1.call-done), kind=kOutput, calls=%fused_computation.4 | convolution fusion | flops 536870912 | bytes 5505024 | tf_op jit(solution)/shard_map/dot_general | solution.py:123
  166.6 1.5 fusion.11
  168.2 0.7 copy-done.3
  168.9 0.7 pad_maximum_fusion.5
  169.9 1.4 broadcast_in_dim.53
  171.3 6.9 %all-to-all-start.2 = ((bf16[8,512,256]{2,1,0:T(8,128)(2,1)}), bf16[8,512,256]{2,1,0:T(8,128)(2,1)S(1)}, u32[]{:S(2)}, u32[]{:S(2)}) async-start(bf16[8,512,256]{2,1,0:T(8,128)(2,1)} %broadcast_in_dim.53), calls=%async_computation.2 | async-start | bytes 4194304 | tf_op jit(solution)/shard_map/all_to_all | solution.py:23
  178.3 3.4 %collective-permute-start.4 = (bf16[2,16,128]{1,2,0:T(8,128)(2,1)S(1)}, bf16[2,16,128]{1,2,0:T(8,128)(2,1)S(1)}, u32[]{:S(2)}, u32[]{:S(2)}) collective-permute-start(bf16[2,16,128]{1,2,0:T(8,128)(2,1)S(1)} %get-tuple-element.28), channel_id=1, source_target_pairs={{0,32},{32,64},{64,96},{96,128},{128,160},{160,192},{192,224},{1,3... | collective-permute-start | bytes 24584 | tf_op jit(solution)/shard_map/ppermute | solution.py:62
  181.7 1.3 collective-permute-start.5
  183.0 39.1 %collective-permute-done.4 = bf16[2,16,128]{1,2,0:T(8,128)(2,1)S(1)} collective-permute-done((bf16[2,16,128]{1,2,0:T(8,128)(2,1)S(1)}, bf16[2,16,128]{1,2,0:T(8,128)(2,1)S(1)}, u32[]{:S(2)}, u32[]{:S(2)}) %collective-permute-start.4) | collective-permute-done | bytes 8224 | tf_op jit(solution)/shard_map/ppermute | solution.py:62
  222.0 4.6 %collective-permute-done.5 = bf16[2,16,128]{1,2,0:T(8,128)(2,1)S(1)} collective-permute-done((bf16[2,16,128]{1,2,0:T(8,128)(2,1)S(1)}, bf16[2,16,128]{1,2,0:T(8,128)(2,1)S(1)}, u32[]{:S(2)}, u32[]{:S(2)}) %collective-permute-start.5) | collective-permute-done | bytes 8224 | tf_op jit(solution)/shard_map/ppermute | solution.py:64
  226.7 6.6 %collective-permute-start.6 = (bf16[2,544,16]{1,2,0:T(8,128)(2,1)S(1)}, bf16[2,544,16]{1,2,0:T(8,128)(2,1)S(1)}, u32[]{:S(2)}, u32[]{:S(2)}) collective-permute-start(bf16[2,544,16]{1,2,0:T(8,128)(2,1)S(1)} %get-tuple-element.24), channel_id=1, source_target_pairs={{0,1},{1,2},{2,3},{3,4},{4,5},{5,6},{6,7},{7,8},{8,9},{9,10},{10,1... | collective-permute-start | bytes 104456 | tf_op jit(solution)/shard_map/ppermute | solution.py:62
  233.3 2.1 collective-permute-start.7
  235.4 5.3 %collective-permute-done.7 = bf16[2,544,16]{1,2,0:T(8,128)(2,1)S(1)} collective-permute-done((bf16[2,544,16]{1,2,0:T(8,128)(2,1)S(1)}, bf16[2,544,16]{1,2,0:T(8,128)(2,1)S(1)}, u32[]{:S(2)}, u32[]{:S(2)}) %collective-permute-start.7) | collective-permute-done | bytes 34848 | tf_op jit(solution)/shard_map/ppermute | solution.py:64
  241.0 4.6 %select_add_fusion = f32[2,512,128]{1,2,0:T(8,128)} fusion(f32[2,544,160]{1,2,0:T(8,128)S(1)} %maximum_convert_fusion.1, s32[]{:T(128)S(6)} %select_n.358, s32[]{:T(128)S(6)} %select_n.359, s32[]{:T(128)S(6)} %select_n.351, s32[]{:T(128)S(6)} %select_n.352, s32[]{:T(128)S(6)} %select_n.344, s32[]{:T(128)S(6)} %select_n.345, s32[]{:T(128)S(6)} %select_n.337, ...), kind=kLoop, calls=%fused_computation.34 | loop fusion | flops 5242880 | bytes 9437256 | tf_op jit(solution)/shard_map/add | solution.py:94
  245.6 4.1 %fusion.2 = f32[512,128]{0,1:T(8,128)} fusion(bf16[4096,128]{1,0:T(8,128)(2,1)} %bitcast.106, bf16[1024,4096]{0,1:T(8,128)(2,1)} %all-gather.8.cloned.1.call-done), kind=kOutput, calls=%fused_computation.2 | convolution fusion | flops 536870912 | bytes 5505024 | tf_op jit(solution)/shard_map/dot_general | solution.py:124
  249.7 4.5 %fusion.17 = f32[512,128]{0,1:T(8,128)} fusion(f32[512,128]{0,1:T(8,128)S(1)} %copy.16, f32[512,128]{0,1:T(8,128)S(1)} %copy-done.6, f32[512,128]{0,1:T(8,128)} %fusion.2, bf16[512,4096]{1,0:T(8,128)(2,1)} %all-gather.4.cloned.1.call-done, bf16[4096,256]{1,0:T(8,128)(2,1)S(1)} %bitcast.99, f32[2,512,128]{1,2,0:T(8,128)S(1)} %copy-done.8, f32[]{:T(128)S(6)} %div.4), kind=kOutput, calls=%fused_computation.21 | convolution fusion | flops 537264128 | bytes 6553604 | tf_op jit(solution)/shard_map/dot_general | solution.py:120
  254.1 1.8 copy.19
  255.9 3.4 %fusion = f32[512,128]{0,1:T(8,128)S(1)} fusion(bf16[4096,128]{1,0:T(8,128)(2,1)} %bitcast.107, bf16[1024,4096]{0,1:T(8,128)(2,1)} %all-gather.8.cloned.1.call-done), kind=kOutput, calls=%fused_computation | convolution fusion | flops 536870912 | bytes 5505024 | tf_op jit(solution)/shard_map/dot_general | solution.py:123
  259.7 1.5 fusion.23
  261.3 0.8 copy.20
  (83 shorter events, 8.4 us)
Async XLA Ops:
  7.2 24.0 %copy-start.12 = (s32[8]{0:T(128)S(1)}, s32[8]{0:T(128)}, u32[]{:S(2)}) copy-start(s32[8]{0:T(128)} %param.10) | copy-start | bytes 100
  7.2 27.3 %copy-start.11 = (f32[8,4096]{1,0:T(8,128)S(1)}, f32[8,4096]{1,0:T(8,128)}, u32[]{:S(2)}) copy-start(f32[8,4096]{1,0:T(8,128)} %param.9) | copy-start | bytes 393220
  7.2 146.9 %all-gather.6.cloned.1.call-start = ((), (), s32[]{:S(2)}) async-start(), calls=%async_computation.4 | async-start | bytes 8650752 | tf_op jit(solution)/shard_map/all_gather | solution.py:47
  10.8 147.4 %all-gather.4.cloned.1.call-start = ((), (), s32[]{:S(2)}) async-start(), calls=%async_computation.3 | async-start | bytes 4325376 | tf_op jit(solution)/shard_map/all_gather | solution.py:116
  14.4 98.6 %collective-permute-start = (bf16[2,16,128]{1,2,0:T(8,128)(2,1)}, bf16[2,16,128]{1,2,0:T(8,128)(2,1)S(1)}, u32[]{:S(2)}, u32[]{:S(2)}) collective-permute-start(bf16[2,16,128]{1,2,0:T(8,128)(2,1)} %get-tuple-element.32), channel_id=1, source_target_pairs={{0,32},{32,64},{64,96},{96,128},{128,160},{160,192},{192,224},{1,3... | collective-permute-start | bytes 24584 | tf_op jit(solution)/shard_map/ppermute | solution.py:62
  18.0 95.0 %collective-permute-start.1 = (bf16[2,16,128]{1,2,0:T(8,128)(2,1)}, bf16[2,16,128]{1,2,0:T(8,128)(2,1)S(1)}, u32[]{:S(2)}, u32[]{:S(2)}) collective-permute-start(bf16[2,16,128]{1,2,0:T(8,128)(2,1)} %get-tuple-element.33), channel_id=1, source_target_pairs={{32,0},{64,32},{96,64},{128,96},{160,128},{192,160},{224,192},{33,... | collective-permute-start | bytes 24584 | tf_op jit(solution)/shard_map/ppermute | solution.py:64
  21.3 58.1 %all-to-all-start.1 = ((bf16[8,512,128]{2,1,0:T(8,128)(2,1)}), bf16[8,512,128]{2,1,0:T(8,128)(2,1)S(1)}, u32[]{:S(2)}, u32[]{:S(2)}) async-start(bf16[8,512,128]{2,1,0:T(8,128)(2,1)} %broadcast_in_dim.49), calls=%async_computation.1 | async-start | bytes 2097152 | tf_op jit(solution)/shard_map/all_to_all | solution.py:23
  79.4 1.6 copy-start.9
  81.1 77.0 %all-to-all-start = ((bf16[8,512,256]{2,1,0:T(8,128)(2,1)}), bf16[8,512,256]{2,1,0:T(8,128)(2,1)S(1)}, u32[]{:S(2)}, u32[]{:S(2)}) async-start(bf16[8,512,256]{2,1,0:T(8,128)(2,1)} %broadcast_in_dim.48), calls=%async_computation | async-start | bytes 4194304 | tf_op jit(solution)/shard_map/all_to_all | solution.py:23
  85.2 160.4 %all-gather.8.cloned.1.call-start = ((), (), s32[]{:S(2)}) async-start(), calls=%async_computation.5 | async-start | bytes 8650752 | tf_op jit(solution)/shard_map/all_gather | solution.py:47
  98.4 63.6 %copy-start.2 = (f32[512,128]{0,1:T(8,128)}, f32[512,128]{0,1:T(8,128)S(1)}, u32[]{:S(2)}) copy-start(f32[512,128]{0,1:T(8,128)S(1)} %get-tuple-element.59) | copy-start | bytes 786436
  113.7 34.8 %collective-permute-start.2 = (bf16[2,544,16]{1,2,0:T(8,128)(2,1)}, bf16[2,544,16]{1,2,0:T(8,128)(2,1)}, u32[]{:S(2)}, u32[]{:S(2)}) collective-permute-start(bf16[2,544,16]{1,2,0:T(8,128)(2,1)} %get-tuple-element.26), channel_id=1, source_target_pairs={{0,1},{1,2},{2,3},{3,4},{4,5},{5,6},{6,7},{7,8},{8,9},{9,10},{10,1... | collective-permute-start | bytes 104456 | tf_op jit(solution)/shard_map/ppermute | solution.py:62
  125.4 23.1 %collective-permute-start.3 = (bf16[2,544,16]{1,2,0:T(8,128)(2,1)}, bf16[2,544,16]{1,2,0:T(8,128)(2,1)}, u32[]{:S(2)}, u32[]{:S(2)}) collective-permute-start(bf16[2,544,16]{1,2,0:T(8,128)(2,1)} %get-tuple-element.27), channel_id=1, source_target_pairs={{1,0},{2,1},{3,2},{4,3},{5,4},{6,5},{7,6},{8,7},{9,8},{10,9},{11,1... | collective-permute-start | bytes 104456 | tf_op jit(solution)/shard_map/ppermute | solution.py:64
  158.1 4.6 %copy-start.10 = (bf16[8,512,128]{2,1,0:T(8,128)(2,1)S(1)}, bf16[8,512,128]{2,1,0:T(8,128)(2,1)}, u32[]{:S(2)}) copy-start(bf16[8,512,128]{2,1,0:T(8,128)(2,1)} %copy-done.9) | copy-start | bytes 3145732
  162.0 0.7 copy-start.5
  162.8 3.9 %copy-start = (bf16[512,4096]{1,0:T(8,128)(2,1)S(1)}, bf16[512,4096]{1,0:T(8,128)(2,1)}, u32[]{:S(2)}) copy-start(bf16[512,4096]{1,0:T(8,128)(2,1)} %all-gather.4.cloned.1.call-done) | copy-start | bytes 12582916
  162.8 3.9 %copy-start.7 = (f32[2,512,128]{1,2,0:T(8,128)S(1)}, f32[2,512,128]{1,2,0:T(8,128)}, u32[]{:S(2)}) copy-start(f32[2,512,128]{1,2,0:T(8,128)} %select_add_fusion.1) | copy-start | bytes 1572868
  168.2 0.7 copy-start.3
  171.3 78.4 %all-to-all-start.2 = ((bf16[8,512,256]{2,1,0:T(8,128)(2,1)}), bf16[8,512,256]{2,1,0:T(8,128)(2,1)S(1)}, u32[]{:S(2)}, u32[]{:S(2)}) async-start(bf16[8,512,256]{2,1,0:T(8,128)(2,1)} %broadcast_in_dim.53), calls=%async_computation.2 | async-start | bytes 4194304 | tf_op jit(solution)/shard_map/all_to_all | solution.py:23
  178.3 43.7 %collective-permute-start.4 = (bf16[2,16,128]{1,2,0:T(8,128)(2,1)S(1)}, bf16[2,16,128]{1,2,0:T(8,128)(2,1)S(1)}, u32[]{:S(2)}, u32[]{:S(2)}) collective-permute-start(bf16[2,16,128]{1,2,0:T(8,128)(2,1)S(1)} %get-tuple-element.28), channel_id=1, source_target_pairs={{0,32},{32,64},{64,96},{96,128},{128,160},{160,192},{192,224},{1,3... | collective-permute-start | bytes 24584 | tf_op jit(solution)/shard_map/ppermute | solution.py:62
  181.7 44.9 %collective-permute-start.5 = (bf16[2,16,128]{1,2,0:T(8,128)(2,1)S(1)}, bf16[2,16,128]{1,2,0:T(8,128)(2,1)S(1)}, u32[]{:S(2)}, u32[]{:S(2)}) collective-permute-start(bf16[2,16,128]{1,2,0:T(8,128)(2,1)S(1)} %get-tuple-element.29), channel_id=1, source_target_pairs={{32,0},{64,32},{96,64},{128,96},{160,128},{192,160},{224,192},{33,... | collective-permute-start | bytes 24584 | tf_op jit(solution)/shard_map/ppermute | solution.py:64
  226.7 8.7 %collective-permute-start.6 = (bf16[2,544,16]{1,2,0:T(8,128)(2,1)S(1)}, bf16[2,544,16]{1,2,0:T(8,128)(2,1)S(1)}, u32[]{:S(2)}, u32[]{:S(2)}) collective-permute-start(bf16[2,544,16]{1,2,0:T(8,128)(2,1)S(1)} %get-tuple-element.24), channel_id=1, source_target_pairs={{0,1},{1,2},{2,3},{3,4},{4,5},{5,6},{6,7},{7,8},{8,9},{9,10},{10,1... | collective-permute-start | bytes 104456 | tf_op jit(solution)/shard_map/ppermute | solution.py:62
  233.3 7.4 %collective-permute-start.7 = (bf16[2,544,16]{1,2,0:T(8,128)(2,1)S(1)}, bf16[2,544,16]{1,2,0:T(8,128)(2,1)S(1)}, u32[]{:S(2)}, u32[]{:S(2)}) collective-permute-start(bf16[2,544,16]{1,2,0:T(8,128)(2,1)S(1)} %get-tuple-element.25), channel_id=1, source_target_pairs={{1,0},{2,1},{3,2},{4,3},{5,4},{6,5},{7,6},{8,7},{9,8},{10,9},{11,1... | collective-permute-start | bytes 104456 | tf_op jit(solution)/shard_map/ppermute | solution.py:64
  245.6 4.1 %copy-start.6 = (f32[512,128]{0,1:T(8,128)S(1)}, f32[512,128]{0,1:T(8,128)}, u32[]{:S(2)}) copy-start(f32[512,128]{0,1:T(8,128)} %copy-done.5) | copy-start | bytes 786436
  245.6 4.1 %copy-start.8 = (f32[2,512,128]{1,2,0:T(8,128)S(1)}, f32[2,512,128]{1,2,0:T(8,128)}, u32[]{:S(2)}) copy-start(f32[2,512,128]{1,2,0:T(8,128)} %select_add_fusion) | copy-start | bytes 1572868
  255.9 3.8 %copy-start.1 = (bf16[512,4096]{1,0:T(8,128)(2,1)S(1)}, bf16[512,4096]{1,0:T(8,128)(2,1)}, u32[]{:S(2)}) copy-start(bf16[512,4096]{1,0:T(8,128)(2,1)} %all-gather.4.cloned.1.call-done) | copy-start | bytes 12582916
  255.9 3.8 %copy-start.4 = (f32[512,128]{0,1:T(8,128)S(1)}, f32[512,128]{0,1:T(8,128)}, u32[]{:S(2)}) copy-start(f32[512,128]{0,1:T(8,128)} %copy-done.3) | copy-start | bytes 786436
Sparse Core Ops, SparseCore 0:
  11.0 66.5 all-gather.5
  80.1 53.4 all-gather.3
  169.8 58.7 all-gather.7
where the time goes:
time: 270 us; the launch traced here: 269 us
  starting transfers between devices  52.8 us (20%)
  waiting for transfers between devices  49.7 us (18%)
  blocking collectives  46.5 us (17%)
  between operations  40.8 us (15%)
  other arithmetic  29.7 us (11%)
  matrix products  26.7 us (10%)
  local copies, waits for them, and re-layouts  22.4 us (8%)
    psum x4, blocking collectives, by_axis(): x = lax.psum(x, axis)  46.5 us
    ppermute x4, waiting for transfers between devices, extended(): lax.ppermute(tail, axis, [(i, (i + 1) % count) for i in range(ends)])  39.1 us
    ppermute x4, starting transfers between devices, extended(): lax.ppermute(tail, axis, [(i, (i + 1) % count) for i in range(ends)])  25.2 us
    all_to_all x3, starting transfers between devices, sent_to_all(): lax.all_to_all(jnp.broadcast_to(x[None], (peers, *x.shape)), axis, 0, 0,...  20.9 us
    ppermute x4, waiting for transfers between devices, extended(): lax.ppermute(head, axis, [((i + 1) % count, i) for i in range(ends)])  9.9 us
    add x2, other arithmetic, dissipate(): summed = summed + jnp.where(jump_slot < active, contribution, 0.0)  9.16 us
    dot_general x2, matrix products, drift(): left_imag = jnp.dot(strip, pieces[1], preferred_element_type=jnp.float32)  8.3 us
    dot_general x2, matrix products, drift(): right_imag = jnp.dot(pieces[1], strip, preferred_element_type=jnp.float32)  8.05 us
  transfers between devices with their start and end apart: 14, of which 3 were waited for; matrix products, arithmetic and copies ran while one was open for 19% of the time, Pallas kernels for 0%

commit v1 on v0

v1 whole, which is shorter than its diff:
```python
import functools

import jax
import jax.numpy as jnp
from jax import lax
from jax.experimental import pallas as pl
from jax.experimental.pallas import tpu as pltpu
from jax.sharding import Mesh
from jax.sharding import PartitionSpec as P

MESH = pl.DeviceIdType.MESH
STEP = 0.25
OMAX = 16
F32 = jnp.float32
BF16 = jnp.bfloat16
NZ, NX, NY, NC = 8, 4, 4, 2
HEIGHT, WIDTH, SLOTS, LEVELS = 512, 128, 8, 4096
BLOCKS = LEVELS // WIDTH
FIRST = (0, 256)
HALF = 128


def iota(shape, dim):
    return lax.broadcasted_iota(jnp.int32, shape, dim)


class Sends:
    def __init__(self, sems):
        self.sems = sems
        self.made = []

    def __call__(self, src, dst, arrived, **device):
        copy = pltpu.make_async_remote_copy(
            src_ref=src,
            dst_ref=dst,
            send_sem=self.sems.at[len(self.made)],
            recv_sem=arrived,
            device_id=device,
            device_id_type=MESH,
        )
        self.made.append(copy)
        copy.start()

    def drain(self):
        for copy in self.made:
            copy.wait_send()


def wait_for(ref, sem):
    pltpu.make_async_copy(ref, ref, sem).wait()


def kernel(
    real, imag, ham, amp, offsets, active, out_real, out_imag,
    row1, row2, col1, col2, part1, part2, acc, peer,
    traces, hs, hr, xe, shifted, onehot, coef, drift1, middle, diss, ts, tx,
    sent, rows1_in, rows2_in, cols1_in, cols2_in, part_in, peer_in, trace_in, halo_in, turn_in,
):
    z, x, y, c = (lax.axis_index(a) for a in ("z", "x", "y", "c"))
    cb = x * 8 + y * 2 + c
    send = Sends(sent)
    other = 1 - c
    near = {
        ("z", 1): lax.rem(z + 1, NZ), ("z", -1): lax.rem(z + NZ - 1, NZ),
        ("x", 1): lax.rem(x + 1, NX), ("x", -1): lax.rem(x + NX - 1, NX),
        ("y", 1): lax.rem(y + 1, NY), ("y", -1): lax.rem(y + NY - 1, NY),
    }

    def quarter(ref, q):
        return ref[pl.ds(pl.multiple_of(q * WIDTH, WIDTH), WIDTH), :]

    class Gather:
        def __init__(self, row, row_in, col, col_in, part, part_sem):
            self.row, self.row_in, self.col, self.col_in = row, row_in, col, col_in
            self.part, self.part_sem = part, part_sem

        def block(self, p, du, dv, h=None):
            dx, dy = (du, dv) if p == 0 else (dv, du)
            if h is None:
                return self.row.at[dx, dy, :, pl.ds(FIRST[p], 2 * HALF), :]
            return self.row.at[dx, dy, :, pl.ds(FIRST[p] + h * HALF, HALF), :]

        def put(self, p, here, there, axis, sign, h=None):
            send(
                self.block(p, *here, h), self.block(p, *there, h),
                self.row_in.at[p, there[0], there[1], h or 0],
                **{axis: near[axis, sign]},
            )

        def arrived(self, p, du, dv, h=None):
            wait_for(self.block(p, du, dv, h), self.row_in.at[p, du, dv, h or 0])

        def along_u(self, p, du, sign, h=None):
            self.put(p, (du, 0), ((du + sign) % 4, 0), "xy"[p], sign, h)

        def along_v(self, p, du, dv, sign, h=None):
            self.put(p, (du, dv), (du, (dv + sign) % 4), "yx"[p], sign, h)

        def source(self, sign, d):
            return lax.rem(z + NZ - sign * d, NZ)

        def piece(self, owner, j):
            return self.col.at[owner, c if j == 0 else other]

        def along_z(self, sign, d, j):
            piece = self.piece(self.source(sign, d), j)
            send(piece, piece, self.col_in.at[(1 - sign) // 2, d, j], z=near["z", sign])

        def arrived_z(self, sign, d, j):
            wait_for(
                self.piece(self.source(sign, d), j), self.col_in.at[(1 - sign) // 2, d - 1, j]
            )
            if d < 3 or (d == 3 and (j == 0) == (sign == 1)):
                self.along_z(sign, d, j)

        def begin(self):
            send(self.part, self.col.at[z, c], self.part_sem, c=other)
            for p in (0, 1):
                for sign in (1, -1):
                    self.along_u(p, 0, sign)
            for sign in (1, -1):
                self.along_z(sign, 0, 0)
            for p in (0, 1):
                for sign in (1, -1):
                    self.along_v(p, 0, 0, sign)
            wait_for(self.col.at[z, other], self.part_sem)
            for sign in (1, -1):
                self.along_z(sign, 0, 1)

        def step_one(self):
            for p in (0, 1):
                for du, sign in ((1, 1), (3, -1)):
                    self.arrived(p, du, 0)
                    self.along_u(p, du, sign, 0 if sign == 1 else 1)
                    for way in (1, -1):
                        self.along_v(p, du, 0, way)
            for j in (0, 1):
                for sign in (1, -1):
                    self.arrived_z(sign, 1, j)
            for p in (0, 1):
                for sign in (1, -1):
                    self.pass_on(p, 0, sign)

        def pass_on(self, p, du, sign):
            dv = 1 if sign == 1 else 3
            self.arrived(p, du, dv)
            self.along_v(p, du, dv, sign, 0 if sign == 1 else 1)

        def step_two(self):
            for p in (0, 1):
                for h in (0, 1):
                    self.arrived(p, 2, 0, h)
                for way in (1, -1):
                    self.along_v(p, 2, 0, way)
            for j in (0, 1):
                for sign in (1, -1):
                    self.arrived_z(sign, 2, j)
            for du in (1, 3):
                for p in (0, 1):
                    for sign in (1, -1):
                        self.pass_on(p, du, sign)

        def step_three(self):
            for j in (0, 1):
                for sign in (1, -1):
                    self.arrived_z(sign, 3, j)
            for p in (0, 1):
                for sign in (1, -1):
                    self.pass_on(p, 2, sign)

        def finish(self):
            for du in (0, 1, 3, 2):
                for p in (0, 1):
                    for h in (0, 1):
                        self.arrived(p, du, 2, h)
            self.arrived_z(1, 4, 0)
            self.arrived_z(-1, 4, 1)

    def trace_over(step, axis, here, count):
        mine = traces.at[step, here]
        for d in range(1, count):
            send(
                mine, mine, trace_in.at[step, d], **{axis: lax.rem(here + d, count)}
            )

    def trace_total(step, here, count):
        for d in range(1, count):
            wait_for(traces.at[step, lax.rem(here + count - d, count)], trace_in.at[step, d])
        total = traces[step, 0]
        for n in range(1, count):
            total = total + traces[step, n]
        return total

    def halo_begin(stage, state):
        turned = jnp.transpose(state)
        hs[stage, 0] = turned[:OMAX, :].astype(BF16)
        hs[stage, 1] = turned[WIDTH - OMAX :, :].astype(BF16)
        xe[stage, OMAX : OMAX + HEIGHT, 0:WIDTH] = state.astype(BF16)
        hr[stage, 2 * OMAX :, :] = jnp.zeros((WIDTH - 2 * OMAX, HEIGHT), BF16)
        for side, step in ((0, BLOCKS - 1), (1, 1)):
            to = lax.rem(cb + step, BLOCKS)
            send(
                hs.at[stage, side], hr.at[stage, pl.ds(side * OMAX, OMAX), :],
                halo_in.at[stage, side],
                x=to // 8, y=lax.rem(to // 2, NY), c=lax.rem(to, NC),
            )

    def halo_rows(stage):
        for side in (0, 1):
            wait_for(hs.at[stage, side], halo_in.at[stage, side])
        xe[stage, OMAX : OMAX + HEIGHT, WIDTH:] = jnp.transpose(hr[stage].astype(F32)).astype(BF16)
        send(
            xe.at[stage, pl.ds(OMAX, OMAX), :], xe.at[stage, pl.ds(OMAX + HEIGHT, OMAX), :],
            halo_in.at[stage, 2], z=near["z", -1],
        )
        send(
            xe.at[stage, pl.ds(HEIGHT, OMAX), :], xe.at[stage, pl.ds(0, OMAX), :],
            halo_in.at[stage, 3], z=near["z", 1],
        )

    def halo_end(stage):
        for side in (2, 3):
            wait_for(xe.at[stage, pl.ds(0, OMAX), :], halo_in.at[stage, side])

    def coefficients():
        count = active[0]
        slot = iota((SLOTS, WIDTH), 0)
        shift = jnp.zeros((SLOTS, WIDTH), jnp.int32)
        for k in range(SLOTS):
            shift = jnp.where(slot == k, offsets[k], shift)

        def strengths(block):
            at = jnp.minimum(jnp.maximum(block, 0), BLOCKS - 1)
            values = amp[:, pl.ds(pl.multiple_of(at * WIDTH, WIDTH), WIDTH)]
            level = block * WIDTH + iota((SLOTS, WIDTH), 1)
            inside = (level >= 0) & (level < LEVELS) & (level + shift >= 0)
            inside = inside & (level + shift < LEVELS) & (slot < count)
            return jnp.where(inside, values, 0.0)

        blocks = [cb] + [4 * z + r for r in range(4)]
        squares = []
        own = []
        for block in blocks:
            window = [strengths(block + d) for d in (-1, 0, 1)]
            own.append(window[1])
            squares.append(jnp.concatenate([w * w for w in window], axis=1))
        squares = jnp.concatenate(squares + [jnp.zeros_like(squares[0])] * 3, axis=0)
        high = squares.astype(BF16)
        rest = squares - high.astype(F32)
        mid = rest.astype(BF16)
        low = (rest - mid.astype(F32)).astype(BF16)
        parts = jnp.concatenate([high, mid, low], axis=0)
        which = lax.rem(iota(parts.shape, 0), SLOTS)
        total = jnp.zeros((parts.shape[0], WIDTH), F32)
        source = iota((3 * WIDTH, WIDTH), 0)
        target = iota((3 * WIDTH, WIDTH), 1)
        for k in range(SLOTS):
            pick = jnp.where(source == target + (WIDTH - offsets[k]), 1.0, 0.0).astype(BF16)
            chosen = jnp.where(which == k, parts.astype(F32), 0.0).astype(BF16)
            total = total + jnp.dot(chosen, pick, preferred_element_type=F32)
        total = total[0:64] + total[64:128] + total[128:192]
        outflow = [jnp.sum(total[8 * n : 8 * n + 8], axis=0, keepdims=True) for n in range(5)]
        coef[0, 0:SLOTS, :] = own[0]
        coef[0, SLOTS : 2 * SLOTS, :] = jnp.broadcast_to(outflow[0], (SLOTS, WIDTH))
        for r in range(4):
            table = jnp.concatenate(
                [
                    own[1 + r],
                    jnp.broadcast_to(outflow[1 + r], (SLOTS, WIDTH)),
                    jnp.zeros((WIDTH - 2 * SLOTS, WIDTH), F32),
                ],
                axis=0,
            )
            coef[1 + r] = jnp.transpose(table)
        source = iota((2 * WIDTH, WIDTH), 0)
        target = iota((2 * WIDTH, WIDTH), 1)
        for k in range(SLOTS):
            at = target + offsets[k]
            at = jnp.where(at < 0, at + (WIDTH + 2 * OMAX), at)
            onehot[:, k * WIDTH : (k + 1) * WIDTH] = jnp.where(source == at, 1.0, 0.0).astype(BF16)

    def dissipator(stage, state):
        shifted[...] = jnp.dot(xe[stage], onehot[...], preferred_element_type=F32)
        for r in range(4):
            rows = slice(r * WIDTH, (r + 1) * WIDTH)
            by_row = coef[1 + r]
            flow = by_row[:, SLOTS : SLOTS + 1] + coef[0, SLOTS : SLOTS + 1, :]
            total = -0.5 * flow * state[rows, :]
            for k in range(SLOTS):
                span = WIDTH + 2 * OMAX
                moved = shifted[r * WIDTH : r * WIDTH + span, k * WIDTH : (k + 1) * WIDTH]
                moved = pltpu.roll(moved, lax.rem(span - OMAX - offsets[k], span), 0)[0:WIDTH]
                total = total + by_row[:, k : k + 1] * coef[0, k : k + 1, :] * moved
            diss[rows, :] = total

    def commutator(stage):
        def add(n, first):
            dx, dy = n // 4, lax.rem(n, 4)
            xk, yk = lax.rem(x + NX - dx, NX), lax.rem(y + NY - dy, NY)
            owner = 2 * xk + yk // 2
            rows = pl.ds(pl.multiple_of(lax.rem(yk, 2) * WIDTH, WIDTH), WIDTH)
            own = row1[dx, dy, 1] if stage == 0 else row2[dx, dy, 0]
            left = jnp.concatenate([own, row1[dx, dy, 0]], axis=1)
            upper = jnp.concatenate([col1[owner, i, 0, rows, :] for i in range(NC)], axis=1)
            if stage == 0:
                lower = [col1[owner, i, 1, rows, :] for i in range(NC)]
            else:
                lower = [col2[owner, i, 0, rows, :] for i in range(NC)]
            right = jnp.concatenate([upper, jnp.concatenate(lower, axis=1)], axis=0)
            for i in range(NC):
                product = jnp.dot(
                    left, right[:, i * WIDTH : (i + 1) * WIDTH], preferred_element_type=F32
                )
                if first:
                    acc[stage, i] = product
                else:
                    acc[stage, i] += product

        add(jnp.int32(0), True)
        lax.fori_loop(1, 16, lambda n, none: (add(n, False), none)[1], 0)
        send(acc.at[stage, other], peer.at[stage], peer_in.at[stage], c=other)
        wait_for(peer.at[stage], peer_in.at[stage])
        return acc[stage, c] + peer[stage]

    def turn_begin(n, value):
        ts[n] = value.astype(BF16)
        for r in range(4):
            stays = (z == cb // 4) & (r == lax.rem(cb, 4))
            src = ts.at[n, pl.ds(r * WIDTH, WIDTH), :]

            def go(r=r, src=src):
                copy = turn_copy(n, r, src)
                copy.start()

            def keep(r=r):
                tx[n, r] = ts[n, r * WIDTH : (r + 1) * WIDTH, :]

            pl.when(jnp.logical_not(stays))(go)
            pl.when(stays)(keep)

    def turn_copy(n, r, src):
        return pltpu.make_async_remote_copy(
            src_ref=src,
            dst_ref=tx.at[n, lax.rem(cb, 4)],
            send_sem=turn_in.at[n, 0, r],
            recv_sem=turn_in.at[n, 1, lax.rem(cb, 4)],
            device_id=dict(z=cb // 4, x=z // 2, y=2 * lax.rem(z, 2) + r // 2, c=jnp.int32(r % 2)),
            device_id_type=MESH,
        )

    def turn_end(n):
        for r in range(4):
            stays = (z == cb // 4) & (r == lax.rem(cb, 4))

            def done(r=r):
                turn_copy(n, r, ts.at[n, pl.ds(r * WIDTH, WIDTH), :]).wait_send()
                wait_for(tx.at[n, r], turn_in.at[n, 1, r])

            pl.when(jnp.logical_not(stays))(done)

    first = Gather(row1, rows1_in, col1, cols1_in, part1, part_in.at[0])
    row1[0, 0, 0] = ham[...]
    row1[0, 0, 1] = (real[...] + imag[...]).astype(BF16)
    for i in range(2):
        rows = slice(i * WIDTH, (i + 1) * WIDTH)
        part1[0, rows, :] = quarter(ham, 2 * i + other)
        part1[1, rows, :] = -quarter(row1.at[0, 0, 1], 2 * i + other)
        col1[z, c, 0, rows, :] = quarter(ham, 2 * i + c)
        col1[z, c, 1, rows, :] = -quarter(row1.at[0, 0, 1], 2 * i + c)
    on_diagonal = iota((HEIGHT, WIDTH), 0) + z * HEIGHT == iota((HEIGHT, WIDTH), 1) + cb * WIDTH
    diagonal = jnp.sum(jnp.where(on_diagonal, real[...], 0.0), axis=0, keepdims=True)
    diagonal = jnp.sum(diagonal, axis=1, keepdims=True)
    traces[0, z] = jnp.broadcast_to(diagonal, (8, WIDTH))
    trace_over(0, "z", z, NZ)
    first.begin()
    halo_begin(0, real[...] - imag[...])
    first.step_one()
    halo_rows(0)
    traces[1, x] = trace_total(0, z, NZ)
    trace_over(1, "x", x, NX)
    coefficients()
    first.step_two()
    traces[2, y] = trace_total(1, x, NX)
    trace_over(2, "y", y, NY)
    halo_end(0)
    first.step_three()
    dissipator(0, real[...] - imag[...])
    first.finish()
    drift1[...] = diss[...] - commutator(0)
    middle[...] = real[...] - imag[...] + STEP * drift1[...]

    second = Gather(row2, rows2_in, col2, cols2_in, part2, part_in.at[1])
    row2[0, 0, 0] = middle[...].astype(BF16)
    for i in range(2):
        rows = slice(i * WIDTH, (i + 1) * WIDTH)
        part2[0, rows, :] = -quarter(row2.at[0, 0, 0], 2 * i + other)
        col2[z, c, 0, rows, :] = -quarter(row2.at[0, 0, 0], 2 * i + c)
    second.begin()
    halo_begin(1, middle[...])
    traces[3, c] = trace_total(2, y, NY)
    trace_over(3, "c", c, NC)
    second.step_one()
    halo_rows(1)
    rescale = jnp.broadcast_to((LEVELS / trace_total(3, c, NC))[0:1, :], (WIDTH, WIDTH))
    rescale = jnp.concatenate([rescale] * 4, axis=0)
    second.step_two()
    halo_end(1)
    second.step_three()
    dissipator(1, middle[...])
    drift1[...] = drift1[...] + rescale * diss[...]
    turn_begin(0, drift1[...])
    second.finish()
    middle[...] = rescale * commutator(1)
    turn_begin(1, middle[...])
    turn_end(0)
    turn_end(1)
    weight = 0.25 * STEP
    for q in range(4):
        rows = slice(q * WIDTH, (q + 1) * WIDTH)
        scale = rescale[rows, :]
        here_x, here_y = drift1[rows, :], middle[rows, :]
        there_x = jnp.transpose(tx[0, q].astype(F32))
        there_y = jnp.transpose(tx[1, q].astype(F32))
        out_real[rows, :] = scale * (
            real[rows, :] + weight * ((here_x + there_x) + (here_y + there_y))
        )
        out_imag[rows, :] = scale * (
            imag[rows, :] + weight * ((there_x - here_x) + (here_y - there_y))
        )
    send.drain()


def local(real, imag, ham, amp, offsets, active):
    vmem = pl.BlockSpec(memory_space=pltpu.VMEM)
    smem = pl.BlockSpec(memory_space=pltpu.SMEM)
    dma = pltpu.SemaphoreType.DMA
    block = jax.ShapeDtypeStruct((HEIGHT, WIDTH), F32)
    return pl.pallas_call(
        kernel,
        out_shape=(block, block),
        in_specs=[vmem, vmem, vmem, vmem, smem, smem],
        out_specs=(vmem, vmem),
        scratch_shapes=[
            pltpu.VMEM((NX, NY, 2, HEIGHT, WIDTH), BF16),
            pltpu.VMEM((NX, NY, 1, HEIGHT, WIDTH), BF16),
            pltpu.VMEM((NZ, NC, 2, 2 * WIDTH, WIDTH), BF16),
            pltpu.VMEM((NZ, NC, 1, 2 * WIDTH, WIDTH), BF16),
            pltpu.VMEM((2, 2 * WIDTH, WIDTH), BF16),
            pltpu.VMEM((1, 2 * WIDTH, WIDTH), BF16),
            pltpu.VMEM((2, NC, HEIGHT, WIDTH), F32),
            pltpu.VMEM((2, HEIGHT, WIDTH), F32),
            pltpu.VMEM((4, NZ, 8, WIDTH), F32),
            pltpu.VMEM((2, 2, OMAX, HEIGHT), BF16),
            pltpu.VMEM((2, WIDTH, HEIGHT), BF16),
            pltpu.VMEM((2, HEIGHT + 2 * OMAX, 2 * WIDTH), BF16),
            pltpu.VMEM((HEIGHT + 2 * OMAX, SLOTS * WIDTH), F32),
            pltpu.VMEM((2 * WIDTH, SLOTS * WIDTH), BF16),
            pltpu.VMEM((5, WIDTH, WIDTH), F32),
            pltpu.VMEM((HEIGHT, WIDTH), F32),
            pltpu.VMEM((HEIGHT, WIDTH), F32),
            pltpu.VMEM((HEIGHT, WIDTH), F32),
            pltpu.VMEM((2, HEIGHT, WIDTH), BF16),
            pltpu.VMEM((2, 4, WIDTH, WIDTH), BF16),
            dma((144,)),
            dma((2, 4, 4, 2)),
            dma((2, 4, 4, 2)),
            dma((2, 4, 2)),
            dma((2, 4, 2)),
            dma((2,)),
            dma((2,)),
            dma((4, NZ)),
            dma((2, 4)),
            dma((2, 2, 4)),
        ],
        compiler_params=pltpu.CompilerParams(
            has_side_effects=True, vmem_limit_bytes=48 * 1024 * 1024
        ),
    )(real, imag, ham, amp, offsets, active)


def solution(mesh):
    split = Mesh(mesh.devices.reshape(NZ, NX, NY, NC), ("z", "x", "y", "c"))
    tiled = P("z", ("x", "y", "c"))
    return jax.shard_map(
        local,
        mesh=split,
        in_specs=(tiled, tiled, tiled, P(), P(), P()),
        out_specs=(tiled, tiled),
        check_vma=False,
    )
```

time: 270 us -> 112 us (0.41)
  the two profiles are of different devices: /device:TPU:25 before, /device:TPU:65 now
where the time goes in v1:
time: 112 us
  Pallas kernels  105 us (94%)
  local copies, waits for them, and re-layouts  5.11 us (5%)
  between operations  1.33 us (1%)
    pallas_call x1, Pallas kernels, local(): pl.pallas_call(kernel, out_shape=(block, block), in_specs=[vmem, vmem, vm...  105 us
    unnamed x12, local copies, waits for them, and re-layouts  5.11 us

profile of v1, /device:TPU:65, one launch (start us, length us, event | category | flops | bytes accessed | tf_op | source)
XLA Modules:
  0.0 111.9 jit_solution(15657246464391537007)
XLA Ops:
  0.6 0.0 copy-start.4
  1.3 0.0 copy-done.4
  1.3 0.0 copy-start
  1.3 0.9 copy-done
  2.3 0.0 copy-start.1
  2.3 0.9 copy-done.1
  3.2 0.0 copy-start.2
  3.2 0.9 copy-done.2
  4.1 0.0 copy-start.3
  4.1 0.9 copy-done.3
  5.0 105.5 %shard_map.77 = (f32[512,128]{1,0:T(8,128)S(1)}, f32[512,128]{1,0:T(8,128)S(1)}) custom-call(f32[512,128]{1,0:T(8,128)S(1)} %copy-done, f32[512,128]{1,0:T(8,128)S(1)} %copy-done.1, bf16[512,128]{1,0:T(8,128)(2,1)S(1)} %copy-done.2, f32[8,4096]{1,0:T(8,128)S(1)} %copy-done.3, s32[8]{0:T(128)S(1)} %copy-done.4, s32[1]{0:T(128)S(6)} %copy.10.active), custom_call_target="tpu_custom_call" | custom-call | tf_op jit(solution)/shard_map/pallas_call | solution.py:438
  110.5 0.7 copy.11
  111.2 0.7 copy.12
Async XLA Ops:
  0.6 0.7 copy-start.4
  1.3 1.0 copy-start
  2.3 0.9 copy-start.1
  3.2 0.9 copy-start.2
  4.1 0.9 copy-start.3

commit v2 on v1

--- a/solution.py
+++ b/solution.py
@@ -51,10 +51,11 @@
 
 
 def kernel(
-    real, imag, ham, amp, offsets, active, out_real, out_imag,
+    real_in, imag_in, ham_in, amp_in, offsets_in, active_in, out_real, out_imag,
+    real, imag, ham, amp, offsets, active, loaded,
     row1, row2, col1, col2, part1, part2, acc, peer,
-    traces, hs, hr, xe, shifted, onehot, coef, drift1, middle, diss, ts, tx,
-    sent, rows1_in, rows2_in, cols1_in, cols2_in, part_in, peer_in, trace_in, halo_in, turn_in,
+    traces, hs, hr, xe, shifted, onehot, coef, drift1, middle, diss, ts, tr, tx,
+    sent, rows1_in, rows2_in, cols1_in, cols2_in, part_in, peer_in, trace_in, halo_in, spread_in, turn_in,
 ):
     z, x, y, c = (lax.axis_index(a) for a in ("z", "x", "y", "c"))
     cb = x * 8 + y * 2 + c
@@ -66,6 +67,23 @@
         ("y", 1): lax.rem(y + 1, NY), ("y", -1): lax.rem(y + NY - 1, NY),
     }
 
+    loads = [
+        pltpu.make_async_copy(src, dst, loaded.at[n])
+        for n, (src, dst) in enumerate(
+            ((ham_in, ham), (real_in, real), (imag_in, imag), (amp_in, amp),
+             (offsets_in, offsets), (active_in, active))
+        )
+    ]
+    for load in loads:
+        load.start()
+    aside = lax.rem(cb + BLOCKS - 1 + 2 * c, BLOCKS)
+    barrier = pltpu.get_barrier_semaphore()
+    greeted = [{axis: at} for (axis, _), at in near.items()] + [
+        dict(c=other), dict(x=aside // 8, y=lax.rem(aside // 2, NY), c=other)
+    ]
+    for device in greeted:
+        pl.semaphore_signal(barrier, inc=1, device_id=device, device_id_type=MESH)
+
     def quarter(ref, q):
         return ref[pl.ds(pl.multiple_of(q * WIDTH, WIDTH), WIDTH), :]
 
@@ -168,13 +186,15 @@
                 for sign in (1, -1):
                     self.pass_on(p, 2, sign)
 
+        def finish_z(self):
+            self.arrived_z(1, 4, 0)
+            self.arrived_z(-1, 4, 1)
+
         def finish(self):
             for du in (0, 1, 3, 2):
                 for p in (0, 1):
                     for h in (0, 1):
                         self.arrived(p, du, 2, h)
-            self.arrived_z(1, 4, 0)
-            self.arrived_z(-1, 4, 1)
 
     def trace_over(step, axis, here, count):
         mine = traces.at[step, here]
@@ -293,72 +313,100 @@
                 total = total + by_row[:, k : k + 1] * coef[0, k : k + 1, :] * moved
             diss[rows, :] = total
 
-    def commutator(stage):
-        def add(n, first):
-            dx, dy = n // 4, lax.rem(n, 4)
-            xk, yk = lax.rem(x + NX - dx, NX), lax.rem(y + NY - dy, NY)
-            owner = 2 * xk + yk // 2
-            rows = pl.ds(pl.multiple_of(lax.rem(yk, 2) * WIDTH, WIDTH), WIDTH)
-            own = row1[dx, dy, 1] if stage == 0 else row2[dx, dy, 0]
-            left = jnp.concatenate([own, row1[dx, dy, 0]], axis=1)
-            upper = jnp.concatenate([col1[owner, i, 0, rows, :] for i in range(NC)], axis=1)
-            if stage == 0:
-                lower = [col1[owner, i, 1, rows, :] for i in range(NC)]
+    def commutator(stage, late):
+        lefts, rights = [], []
+        for dx in range(NX):
+            for dy in range(NY):
+                if (dx == 2 or dy == 2 or (dx, dy) == (3, 3)) != late:
+                    continue
+                xk, yk = lax.rem(x + NX - dx, NX), lax.rem(y + NY - dy, NY)
+                owner = 2 * xk + yk // 2
+                rows = pl.ds(pl.multiple_of(lax.rem(yk, 2) * WIDTH, WIDTH), WIDTH)
+                lefts.append(row1[dx, dy, 1] if stage == 0 else row2[dx, dy, 0])
+                lefts.append(row1[dx, dy, 0])
+                upper = [col1[owner, i, 0, rows, :] for i in range(NC)]
+                if stage == 0:
+                    lower = [col1[owner, i, 1, rows, :] for i in range(NC)]
+                else:
+                    lower = [col2[owner, i, 0, rows, :] for i in range(NC)]
+                rights.append(jnp.concatenate(upper, axis=1))
+                rights.append(jnp.concatenate(lower, axis=1))
+        product = jnp.dot(
+            jnp.concatenate(lefts, axis=1),
+            jnp.concatenate(rights, axis=0),
+            preferred_element_type=F32,
+        )
+        for i in range(NC):
+            mine = product[:, i * WIDTH : (i + 1) * WIDTH]
+            if late:
+                acc[stage, i] += mine
             else:
-                lower = [col2[owner, i, 0, rows, :] for i in range(NC)]
-            right = jnp.concatenate([upper, jnp.concatenate(lower, axis=1)], axis=0)
-            for i in range(NC):
-                product = jnp.dot(
-                    left, right[:, i * WIDTH : (i + 1) * WIDTH], preferred_element_type=F32
-                )
-                if first:
-                    acc[stage, i] = product
-                else:
-                    acc[stage, i] += product
-
-        add(jnp.int32(0), True)
-        lax.fori_loop(1, 16, lambda n, none: (add(n, False), none)[1], 0)
+                acc[stage, i] = mine
+
+    def joined(stage):
         send(acc.at[stage, other], peer.at[stage], peer_in.at[stage], c=other)
         wait_for(peer.at[stage], peer_in.at[stage])
         return acc[stage, c] + peer[stage]
 
-    def turn_begin(n, value):
+    def spread_begin(n, value):
         ts[n] = value.astype(BF16)
-        for r in range(4):
-            stays = (z == cb // 4) & (r == lax.rem(cb, 4))
-            src = ts.at[n, pl.ds(r * WIDTH, WIDTH), :]
-
-            def go(r=r, src=src):
-                copy = turn_copy(n, r, src)
-                copy.start()
-
-            def keep(r=r):
-                tx[n, r] = ts[n, r * WIDTH : (r + 1) * WIDTH, :]
-
-            pl.when(jnp.logical_not(stays))(go)
-            pl.when(stays)(keep)
-
-    def turn_copy(n, r, src):
+        for d in range(1, NX):
+            to = lax.rem(x + d, NX)
+            send(
+                ts.at[n, pl.ds(pl.multiple_of(to * WIDTH, WIDTH), WIDTH), :],
+                tr.at[n, x], spread_in.at[n, d], x=to,
+            )
+        tr[n, x] = ts[n, pl.ds(pl.multiple_of(x * WIDTH, WIDTH), WIDTH), :]
+
+    def turn_copy(n, s):
         return pltpu.make_async_remote_copy(
-            src_ref=src,
+            src_ref=tr.at[n, s],
             dst_ref=tx.at[n, lax.rem(cb, 4)],
-            send_sem=turn_in.at[n, 0, r],
+            send_sem=turn_in.at[n, 0, s],
             recv_sem=turn_in.at[n, 1, lax.rem(cb, 4)],
-            device_id=dict(z=cb // 4, x=z // 2, y=2 * lax.rem(z, 2) + r // 2, c=jnp.int32(r % 2)),
+            device_id=dict(
+                z=2 * s + y // 2, x=z // 2, y=2 * lax.rem(z, 2) + x // 2, c=lax.rem(x, 2)
+            ),
             device_id_type=MESH,
         )
 
+    def turn_stays(s):
+        there = (2 * s + y // 2 == z) & (z // 2 == x)
+        return there & (2 * lax.rem(z, 2) + x // 2 == y) & (lax.rem(x, 2) == c)
+
+    def turn_begin(n):
+        for d in range(1, NX):
+            wait_for(tr.at[n, lax.rem(x + NX - d, NX)], spread_in.at[n, d])
+        for s in range(NX):
+
+            def go(s=s):
+                turn_copy(n, s).start()
+
+            def keep(s=s):
+                tx[n, lax.rem(cb, 4)] = tr[n, s]
+
+            pl.when(jnp.logical_not(turn_stays(s)))(go)
+            pl.when(turn_stays(s))(keep)
+
     def turn_end(n):
-        for r in range(4):
-            stays = (z == cb // 4) & (r == lax.rem(cb, 4))
-
-            def done(r=r):
-                turn_copy(n, r, ts.at[n, pl.ds(r * WIDTH, WIDTH), :]).wait_send()
-                wait_for(tx.at[n, r], turn_in.at[n, 1, r])
-
-            pl.when(jnp.logical_not(stays))(done)
+        for s in range(NX):
+
+            def left(s=s):
+                turn_copy(n, s).wait_send()
+
+            pl.when(jnp.logical_not(turn_stays(s)))(left)
+        for q in range(4):
+            own = (cb // 4 == z) & (2 * lax.rem(z, 2) + q // 2 == y) & (q % 2 == c)
+
+            def arrived(q=q):
+                wait_for(tx.at[n, q], turn_in.at[n, 1, q])
+
+            own = own & (lax.rem(cb, 4) == x)
+            pl.when(jnp.logical_not(own))(arrived)
 
     first = Gather(row1, rows1_in, col1, cols1_in, part1, part_in.at[0])
+    for load in loads[:3]:
+        load.wait()
     row1[0, 0, 0] = ham[...]
     row1[0, 0, 1] = (real[...] + imag[...]).astype(BF16)
     for i in range(2):
@@ -370,23 +418,31 @@
     on_diagonal = iota((HEIGHT, WIDTH), 0) + z * HEIGHT == iota((HEIGHT, WIDTH), 1) + cb * WIDTH
     diagonal = jnp.sum(jnp.where(on_diagonal, real[...], 0.0), axis=0, keepdims=True)
     diagonal = jnp.sum(diagonal, axis=1, keepdims=True)
-    traces[0, z] = jnp.broadcast_to(diagonal, (8, WIDTH))
-    trace_over(0, "z", z, NZ)
+    traces[0, x] = jnp.broadcast_to(diagonal, (8, WIDTH))
+    pl.semaphore_wait(barrier, len(greeted))
     first.begin()
     halo_begin(0, real[...] - imag[...])
     first.step_one()
     halo_rows(0)
-    traces[1, x] = trace_total(0, z, NZ)
-    trace_over(1, "x", x, NX)
+    for load in loads[3:]:
+        load.wait()
     coefficients()
     first.step_two()
-    traces[2, y] = trace_total(1, x, NX)
-    trace_over(2, "y", y, NY)
+    trace_over(0, "x", x, NX)
     halo_end(0)
     first.step_three()
+    traces[1, y] = trace_total(0, x, NX)
+    trace_over(1, "y", y, NY)
     dissipator(0, real[...] - imag[...])
+    first.finish_z()
+    commutator(0, False)
+    traces[2, c] = trace_total(1, y, NY)
+    trace_over(2, "c", c, NC)
     first.finish()
-    drift1[...] = diss[...] - commutator(0)
+    commutator(0, True)
+    traces[3, z] = trace_total(2, c, NC)
+    trace_over(3, "z", z, NZ)
+    drift1[...] = diss[...] - joined(0)
     middle[...] = real[...] - imag[...] + STEP * drift1[...]
 
     second = Gather(row2, rows2_in, col2, cols2_in, part2, part_in.at[1])
@@ -397,50 +453,58 @@
         col2[z, c, 0, rows, :] = -quarter(row2.at[0, 0, 0], 2 * i + c)
     second.begin()
     halo_begin(1, middle[...])
-    traces[3, c] = trace_total(2, y, NY)
-    trace_over(3, "c", c, NC)
     second.step_one()
     halo_rows(1)
-    rescale = jnp.broadcast_to((LEVELS / trace_total(3, c, NC))[0:1, :], (WIDTH, WIDTH))
-    rescale = jnp.concatenate([rescale] * 4, axis=0)
     second.step_two()
     halo_end(1)
     second.step_three()
     dissipator(1, middle[...])
+    rescale = jnp.broadcast_to((LEVELS / trace_total(3, z, NZ))[0:1, :], (WIDTH, WIDTH))
+    rescale = jnp.concatenate([rescale] * 4, axis=0)
     drift1[...] = drift1[...] + rescale * diss[...]
-    turn_begin(0, drift1[...])
+    spread_begin(0, drift1[...])
+    second.finish_z()
+    commutator(1, False)
+    turn_begin(0)
     second.finish()
-    middle[...] = rescale * commutator(1)
-    turn_begin(1, middle[...])
+    commutator(1, True)
+    middle[...] = rescale * joined(1)
+    spread_begin(1, middle[...])
     turn_end(0)
-    turn_end(1)
     weight = 0.25 * STEP
+    turn_begin(1)
     for q in range(4):
         rows = slice(q * WIDTH, (q + 1) * WIDTH)
-        scale = rescale[rows, :]
-        here_x, here_y = drift1[rows, :], middle[rows, :]
-        there_x = jnp.transpose(tx[0, q].astype(F32))
-        there_y = jnp.transpose(tx[1, q].astype(F32))
-        out_real[rows, :] = scale * (
-            real[rows, :] + weight * ((here_x + there_x) + (here_y + there_y))
-        )
-        out_imag[rows, :] = scale * (
-            imag[rows, :] + weight * ((there_x - here_x) + (here_y - there_y))
-        )
+        there = jnp.transpose(tx[0, q].astype(F32))
+        out_real[rows, :] = real[rows, :] + weight * (drift1[rows, :] + there + middle[rows, :])
+        out_imag[rows, :] = imag[rows, :] + weight * (there - drift1[rows, :] + middle[rows, :])
+    turn_end(1)
+    for q in range(4):
+        rows = slice(q * WIDTH, (q + 1) * WIDTH)
+        there = weight * jnp.transpose(tx[1, q].astype(F32))
+        out_real[rows, :] = rescale[rows, :] * (out_real[rows, :] + there)
+        out_imag[rows, :] = rescale[rows, :] * (out_imag[rows, :] - there)
     send.drain()
 
 
 def local(real, imag, ham, amp, offsets, active):
     vmem = pl.BlockSpec(memory_space=pltpu.VMEM)
-    smem = pl.BlockSpec(memory_space=pltpu.SMEM)
+    hbm = pl.BlockSpec(memory_space=pltpu.HBM)
     dma = pltpu.SemaphoreType.DMA
     block = jax.ShapeDtypeStruct((HEIGHT, WIDTH), F32)
     return pl.pallas_call(
         kernel,
         out_shape=(block, block),
-        in_specs=[vmem, vmem, vmem, vmem, smem, smem],
+        in_specs=[hbm] * 6,
         out_specs=(vmem, vmem),
         scratch_shapes=[
+            pltpu.VMEM((HEIGHT, WIDTH), F32),
+            pltpu.VMEM((HEIGHT, WIDTH), F32),
+            pltpu.VMEM((HEIGHT, WIDTH), BF16),
+            pltpu.VMEM((SLOTS, LEVELS), F32),
+            pltpu.SMEM((SLOTS,), jnp.int32),
+            pltpu.SMEM((1,), jnp.int32),
+            dma((6,)),
             pltpu.VMEM((NX, NY, 2, HEIGHT, WIDTH), BF16),
             pltpu.VMEM((NX, NY, 1, HEIGHT, WIDTH), BF16),
             pltpu.VMEM((NZ, NC, 2, 2 * WIDTH, WIDTH), BF16),
@@ -461,7 +525,8 @@
             pltpu.VMEM((HEIGHT, WIDTH), F32),
             pltpu.VMEM((2, HEIGHT, WIDTH), BF16),
             pltpu.VMEM((2, 4, WIDTH, WIDTH), BF16),
-            dma((144,)),
+            pltpu.VMEM((2, 4, WIDTH, WIDTH), BF16),
+            dma((152,)),
             dma((2, 4, 4, 2)),
             dma((2, 4, 4, 2)),
             dma((2, 4, 2)),
@@ -470,10 +535,11 @@
             dma((2,)),
             dma((4, NZ)),
             dma((2, 4)),
+            dma((2, 4)),
             dma((2, 2, 4)),
         ],
         compiler_params=pltpu.CompilerParams(
-            has_side_effects=True, vmem_limit_bytes=48 * 1024 * 1024
+            has_side_effects=True, collective_id=0, vmem_limit_bytes=48 * 1024 * 1024
         ),
     )(real, imag, ham, amp, offsets, active)
 

time: 112 us -> 85.3 us (0.76)
  the two profiles are of different devices: /device:TPU:65 before, /device:TPU:4 now
where the time goes in v2:
time: 85.3 us; the launch traced here: 85.1 us
  Pallas kernels  78.7 us (92%)
  local copies, waits for them, and re-layouts  5.11 us (6%)
  between operations  1.33 us (2%)
    pallas_call x1, Pallas kernels, local(): pl.pallas_call(kernel, out_shape=(block, block), in_specs=[hbm] * 6, out_...  78.7 us
    unnamed x12, local copies, waits for them, and re-layouts  5.11 us

profile of v2, /device:TPU:4, one launch (start us, length us, event | category | flops | bytes accessed | tf_op | source)
XLA Modules:
  0.0 85.1 jit_solution(18411813674479698493)
XLA Ops:
  0.6 0.0 copy-start.4
  1.3 0.0 copy-done.4
  1.3 0.0 copy-start
  1.3 0.9 %copy-done = f32[512,128]{1,0:T(8,128)S(1)} copy-done((f32[512,128]{1,0:T(8,128)S(1)}, f32[512,128]{1,0:T(8,128)}, u32[]{:S(2)}) %copy-start) | copy-done | bytes 262168
  2.3 0.0 copy-start.1
  2.3 0.9 %copy-done.1 = f32[512,128]{1,0:T(8,128)S(1)} copy-done((f32[512,128]{1,0:T(8,128)S(1)}, f32[512,128]{1,0:T(8,128)}, u32[]{:S(2)}) %copy-start.1) | copy-done | bytes 262168
  3.2 0.0 copy-start.2
  3.2 0.9 %copy-done.2 = bf16[512,128]{1,0:T(8,128)(2,1)S(1)} copy-done((bf16[512,128]{1,0:T(8,128)(2,1)S(1)}, bf16[512,128]{1,0:T(8,128)(2,1)}, u32[]{:S(2)}) %copy-start.2) | copy-done | bytes 131096
  4.1 0.0 copy-start.3
  4.1 0.9 %copy-done.3 = f32[8,4096]{1,0:T(8,128)S(1)} copy-done((f32[8,4096]{1,0:T(8,128)S(1)}, f32[8,4096]{1,0:T(8,128)}, u32[]{:S(2)}) %copy-start.3) | copy-done | bytes 131096
  5.0 78.7 %shard_map.77 = (f32[512,128]{1,0:T(8,128)S(1)}, f32[512,128]{1,0:T(8,128)S(1)}) custom-call(f32[512,128]{1,0:T(8,128)S(1)} %copy-done, f32[512,128]{1,0:T(8,128)S(1)} %copy-done.1, bf16[512,128]{1,0:T(8,128)(2,1)S(1)} %copy-done.2, f32[8,4096]{1,0:T(8,128)S(1)} %copy-done.3, s32[8]{0:T(128)S(1)} %copy-done.4, s32[1]{0:T(128)S(6)} %copy.10.active_in), custom_call_target="tpu_custom_call" | custom-call | tf_op jit(solution)/shard_map/pallas_call | solution.py:495
  83.7 0.7 copy.11
  84.4 0.7 copy.12
Async XLA Ops:
  0.6 0.7 copy-start.4
  1.3 1.0 %copy-start = (f32[512,128]{1,0:T(8,128)S(1)}, f32[512,128]{1,0:T(8,128)}, u32[]{:S(2)}) copy-start(f32[512,128]{1,0:T(8,128)} %real_in.1) | copy-start | bytes 786436
  2.3 0.9 %copy-start.1 = (f32[512,128]{1,0:T(8,128)S(1)}, f32[512,128]{1,0:T(8,128)}, u32[]{:S(2)}) copy-start(f32[512,128]{1,0:T(8,128)} %imag_in.1) | copy-start | bytes 786436
  3.2 0.9 %copy-start.2 = (bf16[512,128]{1,0:T(8,128)(2,1)S(1)}, bf16[512,128]{1,0:T(8,128)(2,1)}, u32[]{:S(2)}) copy-start(bf16[512,128]{1,0:T(8,128)(2,1)} %ham_in.1) | copy-start | bytes 393220
  4.1 0.9 %copy-start.3 = (f32[8,4096]{1,0:T(8,128)S(1)}, f32[8,4096]{1,0:T(8,128)}, u32[]{:S(2)}) copy-start(f32[8,4096]{1,0:T(8,128)} %amp_in.1) | copy-start | bytes 393220

commit v3 on v2

v3 whole, which is shorter than its diff:
```python
import functools

import jax
import jax.numpy as jnp
from jax import lax
from jax.experimental import pallas as pl
from jax.experimental.pallas import tpu as pltpu
from jax.sharding import Mesh
from jax.sharding import PartitionSpec as P

MESH = pl.DeviceIdType.MESH
STEP = 0.25
OMAX = 16
F32 = jnp.float32
BF16 = jnp.bfloat16
NZ, NX, NY, NC = 8, 4, 4, 2
HEIGHT, WIDTH, SLOTS, LEVELS = 512, 128, 8, 4096
BLOCKS = LEVELS // WIDTH
FIRST = (0, 256)
HALF = 128


def iota(shape, dim):
    return lax.broadcasted_iota(jnp.int32, shape, dim)


class Sends:
    def __init__(self, sems):
        self.sems = sems

    def __call__(self, group, src, dst, arrived, **device):
        pltpu.make_async_remote_copy(
            src_ref=src,
            dst_ref=dst,
            send_sem=self.sems.at[group],
            recv_sem=arrived,
            device_id=device,
            device_id_type=MESH,
        ).start()

    def drain(self, *totals):
        for group, ref in enumerate(totals):
            wait_for(ref, self.sems.at[group])


def wait_for(ref, sem):
    pltpu.make_async_copy(ref, ref, sem).wait()


def kernel(
    real_in, imag_in, ham_in, amp_in, offsets_in, active_in, next_real, next_imag, next_factor,
    real, imag, ham, amp, offsets, active, loaded, out_real, out_imag, factor, stored,
    row1, row2, col1, col2, part1, part2, acc, peer,
    traces, hs, hr, xe, shifted, onehot, coef, drift1, middle, diss, ts, tr, tx,
    sent, rows1_in, rows2_in, last_in, cols1_in, cols2_in, part_in, peer_in, trace_in, halo_in, spread_in, turn_in,
):
    z, x, y, c = (lax.axis_index(a) for a in ("z", "x", "y", "c"))
    cb = x * 8 + y * 2 + c
    send = Sends(sent)
    other = 1 - c
    near = {
        ("z", 1): lax.rem(z + 1, NZ), ("z", -1): lax.rem(z + NZ - 1, NZ),
        ("x", 1): lax.rem(x + 1, NX), ("x", -1): lax.rem(x + NX - 1, NX),
        ("y", 1): lax.rem(y + 1, NY), ("y", -1): lax.rem(y + NY - 1, NY),
    }

    loads = [
        pltpu.make_async_copy(src, dst, loaded.at[n])
        for n, (src, dst) in enumerate(
            ((ham_in, ham), (real_in, real), (imag_in, imag), (amp_in, amp),
             (offsets_in, offsets), (active_in, active))
        )
    ]
    for load in loads:
        load.start()
    aside = lax.rem(cb + BLOCKS - 1 + 2 * c, BLOCKS)
    barrier = pltpu.get_barrier_semaphore()
    greeted = [{axis: at} for (axis, _), at in near.items()] + [
        dict(c=other), dict(x=aside // 8, y=lax.rem(aside // 2, NY), c=other)
    ]
    for device in greeted:
        pl.semaphore_signal(barrier, inc=1, device_id=device, device_id_type=MESH)

    def quarter(ref, q):
        return ref[pl.ds(pl.multiple_of(q * WIDTH, WIDTH), WIDTH), :]

    class Gather:
        def __init__(self, group, row, row_in, last_in, col, col_in, part, part_sem):
            self.group, self.row, self.row_in, self.last_in = group, row, row_in, last_in
            self.col, self.col_in, self.part, self.part_sem = col, col_in, part, part_sem
            self.arrays = range(part.shape[0])

        def block(self, p, i, du, dv, h=None):
            slot = 4 * du + dv if p == 0 else 4 * dv + du
            first, count = (0, 2 * HALF) if h is None else (h * HALF, HALF)
            return self.row.at[slot, i, pl.ds(FIRST[p] + first, count), :]

        def arrival(self, p, i, du, dv):
            if dv == 2:
                return self.last_in
            if dv == 0:
                return self.row_in.at[i, p, (None, 0, 2, 1)[du]]
            return self.row_in.at[i, p, (3 if dv == 1 else 7) + du]

        def put(self, p, i, here, there, axis, sign, h=None):
            send(
                self.group, self.block(p, i, *here, h), self.block(p, i, *there, h),
                self.arrival(p, i, *there), **{axis: near[axis, sign]},
            )

        def arrived(self, p, i, du, dv):
            wait_for(self.block(p, i, du, dv), self.arrival(p, i, du, dv))

        def along_u(self, p, i, du, sign, h=None):
            self.put(p, i, (du, 0), ((du + sign) % 4, 0), "xy"[p], sign, h)

        def along_v(self, p, i, du, dv, sign, h=None):
            self.put(p, i, (du, dv), (du, (dv + sign) % 4), "yx"[p], sign, h)

        def piece(self, i, sign, d, j):
            owner = lax.rem(z + NZ - sign * d, NZ)
            return self.col.at[owner * NC + (c if j == 0 else other), i]

        def arrival_z(self, i, sign, d, j):
            return self.col_in.at[i, (1 - sign) // 2, min(2 * (d - 1) + j, 6)]

        def along_z(self, i, sign, d, j):
            piece = self.piece(i, sign, d, j)
            send(
                self.group + 1, piece, piece, self.arrival_z(i, sign, d + 1, j),
                z=near["z", sign],
            )

        def arrived_z(self, i, sign, d, j):
            wait_for(self.piece(i, sign, d, j), self.arrival_z(i, sign, d, j))
            if d < 3 or (d == 3 and (j == 0) == (sign == 1)):
                self.along_z(i, sign, d, j)

        def begin(self):
            here = z * NC
            send(self.group + 1, self.part, self.col.at[here + c], self.part_sem, c=other)
            for i in self.arrays:
                for p in (0, 1):
                    for sign in (1, -1):
                        self.along_u(p, i, 0, sign)
                for sign in (1, -1):
                    self.along_z(i, sign, 0, 0)
            for i in self.arrays:
                for p in (0, 1):
                    for sign in (1, -1):
                        self.along_v(p, i, 0, 0, sign)
            wait_for(self.col.at[here + other], self.part_sem)
            for i in self.arrays:
                for sign in (1, -1):
                    self.along_z(i, sign, 0, 1)

        def step_z(self, d, j):
            for i in self.arrays:
                for sign in (1, -1):
                    self.arrived_z(i, sign, d, j)

        def pass_on(self, du):
            for i in self.arrays:
                for p in (0, 1):
                    for sign, dv in ((1, 1), (-1, 3)):
                        self.arrived(p, i, du, dv)
                        self.along_v(p, i, du, dv, sign, 0 if sign == 1 else 1)

        def step_one(self):
            for i in self.arrays:
                for p in (0, 1):
                    for du, sign in ((1, 1), (3, -1)):
                        self.arrived(p, i, du, 0)
                        self.along_u(p, i, du, sign, 0 if sign == 1 else 1)
                        for way in (1, -1):
                            self.along_v(p, i, du, 0, way)
                for sign in (1, -1):
                    self.arrived_z(i, sign, 1, 0)
            self.pass_on(0)
            self.step_z(1, 1)

        def step_two(self):
            for i in self.arrays:
                for p in (0, 1):
                    self.arrived(p, i, 2, 0)
                    for way in (1, -1):
                        self.along_v(p, i, 2, 0, way)
            self.step_z(2, 0)
            self.pass_on(1)
            self.step_z(2, 1)
            self.pass_on(3)

        def step_three(self):
            self.step_z(3, 0)
            self.pass_on(2)
            self.step_z(3, 1)

        def finish_z(self):
            for i in self.arrays:
                self.arrived_z(i, 1, 4, 0)
                self.arrived_z(i, -1, 4, 1)

        def finish(self):
            wait_for(self.row.at[pl.ds(0, 4)], self.last_in)

        def totals(self):
            return self.row.at[pl.ds(0, 15)], self.col.at[pl.ds(0, 15)]

    def trace_over(step, axis, here, count):
        mine = traces.at[step * NZ + here]
        for d in range(1, count):
            send(4, mine, mine, trace_in.at[step], **{axis: lax.rem(here + d, count)})

    def trace_total(step, count):
        wait_for(traces.at[pl.ds(step * NZ, count - 1)], trace_in.at[step])
        total = traces[step * NZ]
        for n in range(1, count):
            total = total + traces[step * NZ + n]
        return total

    def halo_begin(stage, state):
        turned = jnp.transpose(state)
        hs[stage, 0] = turned[:OMAX, :].astype(BF16)
        hs[stage, 1] = turned[WIDTH - OMAX :, :].astype(BF16)
        xe[stage, OMAX : OMAX + HEIGHT, 0:WIDTH] = state.astype(BF16)
        hr[stage, 2 * OMAX :, :] = jnp.zeros((WIDTH - 2 * OMAX, HEIGHT), BF16)
        for side, step in ((0, BLOCKS - 1), (1, 1)):
            to = lax.rem(cb + step, BLOCKS)
            send(
                5, hs.at[stage, side], hr.at[stage, pl.ds(side * OMAX, OMAX), :],
                halo_in.at[stage, 0],
                x=to // 8, y=lax.rem(to // 2, NY), c=lax.rem(to, NC),
            )

    def halo_rows(stage):
        wait_for(hs.at[stage], halo_in.at[stage, 0])
        xe[stage, OMAX : OMAX + HEIGHT, WIDTH:] = jnp.transpose(hr[stage].astype(F32)).astype(BF16)
        send(
            6, xe.at[stage, pl.ds(OMAX, OMAX), :], xe.at[stage, pl.ds(OMAX + HEIGHT, OMAX), :],
            halo_in.at[stage, 1], z=near["z", -1],
        )
        send(
            6, xe.at[stage, pl.ds(HEIGHT, OMAX), :], xe.at[stage, pl.ds(0, OMAX), :],
            halo_in.at[stage, 1], z=near["z", 1],
        )

    def halo_end(stage):
        wait_for(xe.at[stage, pl.ds(0, 2 * OMAX), :], halo_in.at[stage, 1])

    def coefficients():
        count = active[0]
        slot = iota((SLOTS, WIDTH), 0)
        shift = jnp.zeros((SLOTS, WIDTH), jnp.int32)
        for k in range(SLOTS):
            shift = jnp.where(slot == k, offsets[k], shift)

        def strengths(block):
            at = jnp.minimum(jnp.maximum(block, 0), BLOCKS - 1)
            values = amp[:, pl.ds(pl.multiple_of(at * WIDTH, WIDTH), WIDTH)]
            level = block * WIDTH + iota((SLOTS, WIDTH), 1)
            inside = (level >= 0) & (level < LEVELS) & (level + shift >= 0)
            inside = inside & (level + shift < LEVELS) & (slot < count)
            return jnp.where(inside, values, 0.0)

        blocks = [cb] + [4 * z + r for r in range(4)]
        squares = []
        own = []
        for block in blocks:
            window = [strengths(block + d) for d in (-1, 0, 1)]
            own.append(window[1])
            squares.append(jnp.concatenate([w * w for w in window], axis=1))
        squares = jnp.concatenate(squares + [jnp.zeros_like(squares[0])] * 3, axis=0)
        high = squares.astype(BF16)
        rest = squares - high.astype(F32)
        mid = rest.astype(BF16)
        low = (rest - mid.astype(F32)).astype(BF16)
        parts = jnp.concatenate([high, mid, low], axis=0)
        which = lax.rem(iota(parts.shape, 0), SLOTS)
        total = jnp.zeros((parts.shape[0], WIDTH), F32)
        source = iota((3 * WIDTH, WIDTH), 0)
        target = iota((3 * WIDTH, WIDTH), 1)
        for k in range(SLOTS):
            pick = jnp.where(source == target + (WIDTH - offsets[k]), 1.0, 0.0).astype(BF16)
            chosen = jnp.where(which == k, parts.astype(F32), 0.0).astype(BF16)
            total = total + jnp.dot(chosen, pick, preferred_element_type=F32)
        total = total[0:64] + total[64:128] + total[128:192]
        outflow = [jnp.sum(total[8 * n : 8 * n + 8], axis=0, keepdims=True) for n in range(5)]
        coef[0, 0:SLOTS, :] = own[0]
        coef[0, SLOTS : 2 * SLOTS, :] = jnp.broadcast_to(outflow[0], (SLOTS, WIDTH))
        for r in range(4):
            table = jnp.concatenate(
                [
                    own[1 + r],
                    jnp.broadcast_to(outflow[1 + r], (SLOTS, WIDTH)),
                    jnp.zeros((WIDTH - 2 * SLOTS, WIDTH), F32),
                ],
                axis=0,
            )
            coef[1 + r] = jnp.transpose(table)
        source = iota((2 * WIDTH, WIDTH), 0)
        target = iota((2 * WIDTH, WIDTH), 1)
        for k in range(SLOTS):
            at = target + offsets[k]
            at = jnp.where(at < 0, at + (WIDTH + 2 * OMAX), at)
            onehot[:, k * WIDTH : (k + 1) * WIDTH] = jnp.where(source == at, 1.0, 0.0).astype(BF16)

    def dissipator(stage, state):
        shifted[...] = jnp.dot(xe[stage], onehot[...], preferred_element_type=F32)
        for r in range(4):
            rows = slice(r * WIDTH, (r + 1) * WIDTH)
            by_row = coef[1 + r]
            flow = by_row[:, SLOTS : SLOTS + 1] + coef[0, SLOTS : SLOTS + 1, :]
            total = -0.5 * flow * state[rows, :]
            for k in range(SLOTS):
                span = WIDTH + 2 * OMAX
                moved = shifted[r * WIDTH : r * WIDTH + span, k * WIDTH : (k + 1) * WIDTH]
                moved = pltpu.roll(moved, lax.rem(span - OMAX - offsets[k], span), 0)[0:WIDTH]
                total = total + by_row[:, k : k + 1] * coef[0, k : k + 1, :] * moved
            diss[rows, :] = total

    def commutator(stage, late):
        lefts, rights = [], []
        for dx in range(NX):
            for dy in range(NY):
                if (dx == 2 or dy == 2 or (dx, dy) == (3, 3)) != late:
                    continue
                xk, yk = lax.rem(x + NX - dx, NX), lax.rem(y + NY - dy, NY)
                owner = NC * (2 * xk + yk // 2)
                slot = 4 * dx + dy
                rows = pl.ds(pl.multiple_of(lax.rem(yk, 2) * WIDTH, WIDTH), WIDTH)
                lefts.append(row1[slot, 1] if stage == 0 else row2[slot, 0])
                lefts.append(row1[slot, 0])
                upper = [col1[owner + i, 0, rows, :] for i in range(NC)]
                if stage == 0:
                    lower = [col1[owner + i, 1, rows, :] for i in range(NC)]
                else:
                    lower = [col2[owner + i, 0, rows, :] for i in range(NC)]
                rights.append(jnp.concatenate(upper, axis=1))
                rights.append(jnp.concatenate(lower, axis=1))
        product = jnp.dot(
            jnp.concatenate(lefts, axis=1),
            jnp.concatenate(rights, axis=0),
            preferred_element_type=F32,
        )
        for i in range(NC):
            mine = product[:, i * WIDTH : (i + 1) * WIDTH]
            if late:
                acc[stage, i] += mine
            else:
                acc[stage, i] = mine

    def joined(stage):
        send(7, acc.at[stage, other], peer.at[stage], peer_in.at[stage], c=other)
        wait_for(peer.at[stage], peer_in.at[stage])
        return acc[stage, c] + peer[stage]

    def spread_begin(n, value):
        ts[n] = value.astype(BF16)
        for d in range(1, NX):
            to = lax.rem(x + d, NX)
            send(
                8, ts.at[n, pl.ds(pl.multiple_of(to * WIDTH, WIDTH), WIDTH), :],
                tr.at[4 * n + x], spread_in.at[n, d - 1], x=to,
            )
        tr[4 * n + x] = ts[n, pl.ds(pl.multiple_of(x * WIDTH, WIDTH), WIDTH), :]

    def turn_copy(n, s):
        return pltpu.make_async_remote_copy(
            src_ref=tr.at[4 * n + s],
            dst_ref=tx.at[n, lax.rem(cb, 4)],
            send_sem=turn_in.at[n, 0, s],
            recv_sem=turn_in.at[n, 1, lax.rem(cb, 4)],
            device_id=dict(
                z=2 * s + y // 2, x=z // 2, y=2 * lax.rem(z, 2) + x // 2, c=lax.rem(x, 2)
            ),
            device_id_type=MESH,
        )

    def turn_stays(s):
        there = (2 * s + y // 2 == z) & (z // 2 == x)
        return there & (2 * lax.rem(z, 2) + x // 2 == y) & (lax.rem(x, 2) == c)

    def turn_begin(n):
        for d in (0, 1, 3, 2):
            s = lax.rem(x + NX - d, NX)
            if d:
                wait_for(tr.at[4 * n + s], spread_in.at[n, d - 1])

            def go(s=s):
                turn_copy(n, s).start()

            def keep(s=s):
                tx[n, lax.rem(cb, 4)] = tr[4 * n + s]

            pl.when(jnp.logical_not(turn_stays(s)))(go)
            pl.when(turn_stays(s))(keep)

    def turn_sent(n):
        for s in range(NX):

            def left(s=s):
                turn_copy(n, s).wait_send()

            pl.when(jnp.logical_not(turn_stays(s)))(left)

    def turn_arrived(n, q):
        own = (cb // 4 == z) & (2 * lax.rem(z, 2) + q // 2 == y) & (q % 2 == c)
        own = own & (lax.rem(cb, 4) == x)
        pl.when(jnp.logical_not(own))(lambda: wait_for(tx.at[n, q], turn_in.at[n, 1, q]))

    first = Gather(0, row1, rows1_in, last_in.at[0], col1, cols1_in, part1, part_in.at[0])
    for load in loads[:3]:
        load.wait()
    row1[0, 0] = ham[...]
    row1[0, 1] = (real[...] + imag[...]).astype(BF16)
    for i in range(2):
        rows = slice(i * WIDTH, (i + 1) * WIDTH)
        part1[0, rows, :] = quarter(ham, 2 * i + other)
        part1[1, rows, :] = -quarter(row1.at[0, 1], 2 * i + other)
        col1[z * NC + c, 0, rows, :] = quarter(ham, 2 * i + c)
        col1[z * NC + c, 1, rows, :] = -quarter(row1.at[0, 1], 2 * i + c)
    on_diagonal = iota((HEIGHT, WIDTH), 0) + z * HEIGHT == iota((HEIGHT, WIDTH), 1) + cb * WIDTH
    diagonal = jnp.sum(jnp.where(on_diagonal, real[...], 0.0), axis=0, keepdims=True)
    diagonal = jnp.sum(diagonal, axis=1, keepdims=True)
    traces[x] = jnp.broadcast_to(diagonal, (8, WIDTH))
    pl.semaphore_wait(barrier, len(greeted))
    first.begin()
    halo_begin(0, real[...] - imag[...])
    first.step_one()
    halo_rows(0)
    for load in loads[3:]:
        load.wait()
    coefficients()
    first.step_two()
    trace_over(0, "x", x, NX)
    halo_end(0)
    dissipator(0, real[...] - imag[...])
    first.step_three()
    traces[NZ + y] = trace_total(0, NX)
    trace_over(1, "y", y, NY)
    first.finish_z()
    commutator(0, False)
    traces[2 * NZ + c] = trace_total(1, NY)
    trace_over(2, "c", c, NC)
    first.finish()
    commutator(0, True)
    traces[3 * NZ + z] = trace_total(2, NC)
    trace_over(3, "z", z, NZ)
    drift1[...] = diss[...] - joined(0)
    middle[...] = real[...] - imag[...] + STEP * drift1[...]

    second = Gather(2, row2, rows2_in, last_in.at[1], col2, cols2_in, part2, part_in.at[1])
    row2[0, 0] = middle[...].astype(BF16)
    for i in range(2):
        rows = slice(i * WIDTH, (i + 1) * WIDTH)
        part2[0, rows, :] = -quarter(row2.at[0, 0], 2 * i + other)
        col2[z * NC + c, 0, rows, :] = -quarter(row2.at[0, 0], 2 * i + c)
    second.begin()
    halo_begin(1, middle[...])
    second.step_one()
    halo_rows(1)
    second.step_two()
    halo_end(1)
    dissipator(1, middle[...])
    rescale = LEVELS / trace_total(3, NZ)
    factor[...] = rescale
    rescale = jnp.concatenate([rescale] * (HEIGHT // 8), axis=0)
    drift1[...] = drift1[...] + rescale * diss[...]
    spread_begin(0, drift1[...])
    second.step_three()
    second.finish_z()
    commutator(1, False)
    turn_begin(0)
    second.finish()
    commutator(1, True)
    middle[...] = rescale * joined(1)
    spread_begin(1, middle[...])
    turn_begin(1)
    weight = 0.25 * STEP
    for q in range(4):
        rows = slice(q * WIDTH, (q + 1) * WIDTH)
        turn_arrived(0, q)
        there = jnp.transpose(tx[0, q].astype(F32))
        out_real[rows, :] = real[rows, :] + weight * (drift1[rows, :] + there + middle[rows, :])
        out_imag[rows, :] = imag[rows, :] + weight * (there - drift1[rows, :] + middle[rows, :])
    pltpu.make_async_copy(factor, next_factor, stored.at[2]).start()
    for q in range(4):
        rows = slice(q * WIDTH, (q + 1) * WIDTH)
        turn_arrived(1, q)
        there = weight * jnp.transpose(tx[1, q].astype(F32))
        out_real[rows, :] = out_real[rows, :] + there
        out_imag[rows, :] = out_imag[rows, :] - there
        for n, (out, to) in enumerate(((out_real, next_real), (out_imag, next_imag))):
            pltpu.make_async_copy(out.at[rows, :], to.at[rows, :], stored.at[n]).start()
    turn_sent(0)
    turn_sent(1)
    send.drain(
        *first.totals(), *second.totals(), traces.at[pl.ds(0, 14)], hs,
        xe.at[0, pl.ds(0, 4 * OMAX), :], peer, tr.at[pl.ds(0, 6)],
    )
    wait_for(factor, stored.at[2])
    wait_for(out_real, stored.at[0])
    wait_for(out_imag, stored.at[1])


def local(real, imag, ham, amp, offsets, active):
    hbm = pl.BlockSpec(memory_space=pltpu.HBM)
    dma = pltpu.SemaphoreType.DMA
    block = jax.ShapeDtypeStruct((HEIGHT, WIDTH), F32)
    next_real, next_imag, factor = pl.pallas_call(
        kernel,
        out_shape=(block, block, jax.ShapeDtypeStruct((8, WIDTH), F32)),
        in_specs=[hbm] * 6,
        out_specs=(hbm, hbm, hbm),
        scratch_shapes=[
            pltpu.VMEM((HEIGHT, WIDTH), F32),
            pltpu.VMEM((HEIGHT, WIDTH), F32),
            pltpu.VMEM((HEIGHT, WIDTH), BF16),
            pltpu.VMEM((SLOTS, LEVELS), F32),
            pltpu.SMEM((SLOTS,), jnp.int32),
            pltpu.SMEM((1,), jnp.int32),
            dma((6,)),
            pltpu.VMEM((HEIGHT, WIDTH), F32),
            pltpu.VMEM((HEIGHT, WIDTH), F32),
            pltpu.VMEM((8, WIDTH), F32),
            dma((3,)),
            pltpu.VMEM((NX * NY, 2, HEIGHT, WIDTH), BF16),
            pltpu.VMEM((NX * NY, 1, HEIGHT, WIDTH), BF16),
            pltpu.VMEM((NZ * NC, 2, 2 * WIDTH, WIDTH), BF16),
            pltpu.VMEM((NZ * NC, 1, 2 * WIDTH, WIDTH), BF16),
            pltpu.VMEM((2, 2 * WIDTH, WIDTH), BF16),
            pltpu.VMEM((1, 2 * WIDTH, WIDTH), BF16),
            pltpu.VMEM((2, NC, HEIGHT, WIDTH), F32),
            pltpu.VMEM((2, HEIGHT, WIDTH), F32),
            pltpu.VMEM((4 * NZ, 8, WIDTH), F32),
            pltpu.VMEM((2, 2, OMAX, HEIGHT), BF16),
            pltpu.VMEM((2, WIDTH, HEIGHT), BF16),
            pltpu.VMEM((2, HEIGHT + 2 * OMAX, 2 * WIDTH), BF16),
            pltpu.VMEM((HEIGHT + 2 * OMAX, SLOTS * WIDTH), F32),
            pltpu.VMEM((2 * WIDTH, SLOTS * WIDTH), BF16),
            pltpu.VMEM((5, WIDTH, WIDTH), F32),
            pltpu.VMEM((HEIGHT, WIDTH), F32),
            pltpu.VMEM((HEIGHT, WIDTH), F32),
            pltpu.VMEM((HEIGHT, WIDTH), F32),
            pltpu.VMEM((2, HEIGHT, WIDTH), BF16),
            pltpu.VMEM((8, WIDTH, WIDTH), BF16),
            pltpu.VMEM((2, 4, WIDTH, WIDTH), BF16),
            dma((9,)),
            dma((2, 2, 11)),
            dma((1, 2, 11)),
            dma((2,)),
            dma((2, 2, 7)),
            dma((1, 2, 7)),
            dma((2,)),
            dma((2,)),
            dma((4,)),
            dma((2, 2)),
            dma((2, 3)),
            dma((2, 2, 4)),
        ],
        compiler_params=pltpu.CompilerParams(
            has_side_effects=True, collective_id=0, vmem_limit_bytes=63 * 1024 * 1024
        ),
    )(real, imag, ham, amp, offsets, active)
    return next_real * factor[0, 0], next_imag * factor[0, 0]


def solution(mesh):
    split = Mesh(mesh.devices.reshape(NZ, NX, NY, NC), ("z", "x", "y", "c"))
    tiled = P("z", ("x", "y", "c"))
    return jax.shard_map(
        local,
        mesh=split,
        in_specs=(tiled, tiled, tiled, P(), P(), P()),
        out_specs=(tiled, tiled),
        check_vma=False,
    )
```

time: 85.3 us -> 79.4 us (0.931)
  the two profiles are of different devices: /device:TPU:4 before, /device:TPU:8 now
where the time goes in v3:
time: 79.4 us; the launch traced here: 79.2 us
  Pallas kernels  74.2 us (93%)
  other arithmetic  2.46 us (3%)
  between operations  1.29 us (2%)
  local copies, waits for them, and re-layouts  1.23 us (2%)
    pallas_call x1, Pallas kernels, local(): pl.pallas_call(kernel, out_shape=(block, block, jax.ShapeDtypeStruct((8,...  74.2 us
    mul x1, other arithmetic, local(): return (next_real * factor[0, 0], next_imag * factor[0, 0])  2.46 us

profile of v3, /device:TPU:8, one launch (start us, length us, event | category | flops | bytes accessed | tf_op | source)
XLA Modules:
  0.0 79.2 jit_solution(18159227681743124287)
XLA Ops:
  1.3 74.2 %shard_map.77 = (f32[512,128]{1,0:T(8,128)}, f32[512,128]{1,0:T(8,128)}, f32[8,128]{1,0:T(8,128)}) custom-call(f32[512,128]{1,0:T(8,128)} %real_in.1, f32[512,128]{1,0:T(8,128)} %imag_in.1, bf16[512,128]{1,0:T(8,128)(2,1)} %ham_in.1, f32[8,4096]{1,0:T(8,128)} %amp_in.1, s32[8]{0:T(128)} %offsets_in.1, s32[1]{0:T(128)S(6)} %copy.8.active_in), custom_call_target="tpu_custom_call" | custom-call | tf_op jit(solution)/shard_map/pallas_call | solution.py:510
  75.5 1.2 %slice.4 = f32[1,1]{1,0:T(1,128)} slice(f32[8,128]{1,0:T(8,128)} %get-tuple-element.6), slice={[0:1], [0:1]} | slice | bytes 8 | tf_op jit(solution)/shard_map/slice | solution.py:565
  76.7 2.5 %broadcast_multiply_fusion = (f32[512,128]{1,0:T(8,128)}, f32[512,128]{1,0:T(8,128)}) fusion(f32[512,128]{1,0:T(8,128)} %get-tuple-element.7, f32[]{:T(128)} %bitcast, f32[512,128]{1,0:T(8,128)} %get-tuple-element.5), kind=kLoop, calls=%fused_computation | loop fusion | flops 131072 | bytes 1048580 | tf_op jit(solution)/shard_map/mul | solution.py:565
